TPU v7x, 32 devices: a whole 2x2x4 slice. The times are simulated.
32 devices in a mesh: rows: 8 (over y, x, core), cols: 4 (over z).
Axes of the slice: x: 2, y: 2, z: 4, core: 2. Of those that a mesh axis runs over, the one named last changes fastest.
Arguments:
- token_ids: int32 [16, 2048], P('rows', 'cols'), may hold values from 0 to 131071, as said below
- lengths: int32 [16], P('rows'), may hold values from 1 to 2048
- table: bfloat16 [131072, 512], P('rows', 'cols'), may hold values from -6 to 6
- attn_gain: float32 [512], replicated, may hold values from 0.1 to 1.9
- w_qkv: bfloat16 [512, 1536], replicated, may hold values from -2 to 2
- w_out: bfloat16 [512, 512], replicated, may hold values from -0.25 to 0.25
- mlp_gain: float32 [512], replicated, may hold values from 0.1 to 1.9
- w_in: bfloat16 [512, 4096], replicated, may hold values from -0.25 to 0.25
- w_down: bfloat16 [2048, 512], replicated, may hold values from -0.125 to 0.125
Outputs:
- layer_out: bfloat16 [16, 2048, 512], P('rows', 'cols')
Inputs may be any that keep to these rules, and one draw needn't show every extreme that they name: `token_ids`: ids lie in 0 to 131071. In each aligned block of 2 histories (4096 positions) at most 1365 ids fall in any one block of 16384 consecutive table rows, and in every such block of histories some block of table rows receives exactly 1365.
All inputs are finite; a program needn't handle non-finite values.
Results may differ from a plain program's by a relative error of at most 0.012.
Values may be sent and summed in bfloat16 or wider, within the bound.
A program may use at most 192 MiB of HBM per device.

v0:
```python
import functools

import jax
import jax.numpy as jnp
from jax import lax
from jax.experimental import pallas as pl
from jax.experimental.pallas import tpu as pltpu
from jax.sharding import PartitionSpec as P

HEADS = 8
LANES = 128
NEG = -1e30
SCORE_SCALE = 0.125 * 1.4426950408889634
MESH = pl.DeviceIdType.MESH
BF = jnp.bfloat16
F32 = jnp.float32


def rms_norm(values_f32, gain):
    mean_sq = jnp.mean(values_f32 * values_f32, axis=-1, keepdims=True)
    return values_f32 * lax.rsqrt(mean_sq + 1e-06) * gain


def layer_kernel(
    cols, lens_ref, e_ref, gain1, gain2, wq_h, wk_h, wv_h, wo_h, wi_h, wd_h, out_ref,
    ebuf, wq, wk, wv, wo, wi, wd, qm, k_s, v_s, m_s, l_s, acc,
    send_sem, recv_sem, own_sem, w_sem,
):
    me = lax.axis_index("cols")
    batch, full, width = e_ref.shape
    quarter = full // cols
    head_dim = LANES // 2

    def chunk(j):
        return pl.ds(pl.multiple_of(j * quarter, quarter), quarter)

    def slice_copy(b, source, target, j):
        return pltpu.make_async_remote_copy(
            src_ref=e_ref.at[b, chunk(j)],
            dst_ref=ebuf.at[source, b, chunk(j)],
            send_sem=send_sem.at[b, target, j],
            recv_sem=recv_sem.at[b, source, j],
            device_id={"cols": target},
            device_id_type=MESH,
        )

    barrier = pltpu.get_barrier_semaphore()
    for off in range(1, cols):
        pl.semaphore_signal(
            barrier, inc=1, device_id={"cols": lax.rem(me + off, cols)}, device_id_type=MESH
        )
    pl.semaphore_wait(barrier, cols - 1)

    def for_sends(act):
        def step(i, carry):
            b, t = i // cols, lax.rem(i, cols)
            for d in reversed(range(cols)):
                j = jnp.where(t == 0, d, t - 1)

                @pl.when((me != d) & (t <= d))
                def _():
                    act(slice_copy(b, me, d, j))

            return carry

        lax.fori_loop(0, batch * cols, step, 0)

    for_sends(lambda copy: copy.start())
    own = pltpu.make_async_copy(e_ref, ebuf.at[me], own_sem)
    own.start()
    loads = [
        pltpu.make_async_copy(src, dst, w_sem.at[i])
        for i, (src, dst) in enumerate(
            ((wq_h, wq), (wk_h, wk), (wv_h, wv), (wo_h, wo), (wi_h, wi), (wd_h, wd))
        )
    ]
    for load in loads:
        load.start()
    own.wait()
    for load in loads:
        load.wait()

    dims_nt = (((1,), (1,)), ((), ()))

    def embedded(b, j):
        parts = [ebuf[s, b, chunk(j), :] for s in range(cols)]
        return jnp.concatenate(parts, axis=1).astype(F32)

    def history(b, carry):
        length = lens_ref[b]
        query_pos = me * quarter + lax.broadcasted_iota(jnp.int32, (1, quarter), 1)
        limit = jnp.minimum(query_pos + 1, length)

        def unit(t, carry):
            j = jnp.where(t == 0, me, t - 1)
            for s in range(cols):

                @pl.when(me != s)
                def _():
                    slice_copy(b, s, s, j).wait_recv()

            normed = rms_norm(embedded(b, j), gain1[...]).astype(BF)
            k_s[...] = jnp.dot(normed, wk[...], preferred_element_type=F32).astype(BF)
            v_s[...] = lax.dot_general(
                wv[...], normed, dims_nt, preferred_element_type=F32
            ).astype(BF)

            @pl.when(t == 0)
            def _():
                q_t = lax.dot_general(
                    wq[...], normed, dims_nt, preferred_element_type=F32
                ).astype(BF)
                zero = jnp.zeros((head_dim, quarter), BF)
                for h in range(HEADS):
                    mine = q_t[h * head_dim : (h + 1) * head_dim]
                    pair = (mine, zero) if h % 2 == 0 else (zero, mine)
                    qm[h] = jnp.concatenate(pair, axis=0)
                m_s[...] = jnp.full_like(m_s, NEG)
                l_s[...] = jnp.zeros_like(l_s)
                acc[...] = jnp.zeros_like(acc)

            key_pos = lax.broadcasted_iota(jnp.int32, (quarter, quarter), 0)
            keep = key_pos < limit - j * quarter

            def pair(p, carry):
                k_pair = k_s[:, pl.ds(pl.multiple_of(p * LANES, LANES), LANES)]
                for side in range(2):
                    h = 2 * p + side
                    s = jnp.dot(k_pair, qm[h], preferred_element_type=F32) * SCORE_SCALE
                    s = jnp.where(keep, s, NEG)
                    m_old = m_s[h]
                    m_new = jnp.maximum(m_old, jnp.max(s, axis=0, keepdims=True))
                    probs = jnp.exp2(s - m_new)
                    alpha = jnp.exp2(m_old - m_new)
                    m_s[h] = m_new
                    l_s[h] = l_s[h] * alpha + jnp.sum(probs, axis=0, keepdims=True)
                    v_t = v_s[pl.ds(pl.multiple_of(h * head_dim, head_dim), head_dim), :]
                    acc[h] = acc[h] * alpha + jnp.dot(
                        v_t, probs.astype(BF), preferred_element_type=F32
                    )
                return carry

            lax.fori_loop(0, HEADS // 2, pair, 0)
            return carry

        lax.fori_loop(0, me + 1, unit, 0)

        att_t = (acc[...] / l_s[...]).reshape(HEADS * head_dim, quarter)
        attended = att_t.T.astype(BF)
        hidden = (
            embedded(b, me) + jnp.dot(attended, wo[...], preferred_element_type=F32)
        ).astype(BF)
        hidden = hidden.astype(F32)
        normed_two = rms_norm(hidden, gain2[...]).astype(BF)
        ff = wd.shape[0]
        tile = 512
        total = hidden
        for f in range(0, ff, tile):
            gate = jnp.dot(normed_two, wi[:, f : f + tile], preferred_element_type=F32)
            up = jnp.dot(normed_two, wi[:, ff + f : ff + f + tile], preferred_element_type=F32)
            act = (gate / (1.0 + jnp.exp(-gate)) * up).astype(BF)
            total = total + jnp.dot(act, wd[f : f + tile, :], preferred_element_type=F32)
        out_ref[b] = total.astype(BF)
        return carry

    lax.fori_loop(0, batch, history, 0)
    for_sends(lambda copy: copy.wait_send())


def layer_call(cols, lengths, emb, gain1, gain2, w_qkv, w_out, w_in, w_down):
    batch, full, width = emb.shape
    quarter = full // cols
    d = width * cols
    wq_t = w_qkv[:, :d].T
    wk = w_qkv[:, d : 2 * d]
    wv_t = w_qkv[:, 2 * d :].T
    any_spec = pl.BlockSpec(memory_space=pl.ANY)
    vmem = pl.BlockSpec(memory_space=pltpu.VMEM)
    smem = pl.BlockSpec(memory_space=pltpu.SMEM)
    weights = (wq_t, wk, wv_t, w_out, w_in, w_down)
    head_dim = d // HEADS
    return pl.pallas_call(
        functools.partial(layer_kernel, cols),
        out_shape=jax.ShapeDtypeStruct((batch, quarter, d), BF),
        in_specs=[smem, any_spec, vmem, vmem] + [any_spec] * 6,
        out_specs=vmem,
        scratch_shapes=[pltpu.VMEM((cols, batch, full, width), BF)]
        + [pltpu.VMEM(w.shape, BF) for w in weights]
        + [
            pltpu.VMEM((HEADS, 2 * head_dim, quarter), BF),
            pltpu.VMEM((quarter, d), BF),
            pltpu.VMEM((d, quarter), BF),
            pltpu.VMEM((HEADS, 1, quarter), F32),
            pltpu.VMEM((HEADS, 1, quarter), F32),
            pltpu.VMEM((HEADS, head_dim, quarter), F32),
            pltpu.SemaphoreType.DMA((batch, cols, cols)),
            pltpu.SemaphoreType.DMA((batch, cols, cols)),
            pltpu.SemaphoreType.DMA,
            pltpu.SemaphoreType.DMA((6,)),
        ],
        compiler_params=pltpu.CompilerParams(
            collective_id=0, has_side_effects=True, vmem_limit_bytes=60 * 1024 * 1024
        ),
    )(lengths, emb, gain1.reshape(1, d), gain2.reshape(1, d), *weights)


def local(token_ids, lengths, table, attn_gain, w_qkv, w_out, mlp_gain, w_in, w_down):
    batch_dev, quarter = token_ids.shape
    col_count = lax.axis_size("cols")
    row_count = lax.axis_size("rows")
    full_len = quarter * col_count
    block_rows, col_width = table.shape
    own_ids = lax.all_gather(token_ids, "cols", axis=1, tiled=True)
    flat_ids = own_ids.reshape(-1)
    token_count = flat_ids.shape[0]
    capacity = -(-(8 * token_count // (3 * row_count)) // 16) * 16
    owner_block = flat_ids // block_rows
    offset = flat_ids - owner_block * block_rows
    onehot = (owner_block[:, None] == jnp.arange(row_count, dtype=jnp.int32)[None, :]).astype(
        jnp.int32
    )
    slot_rank = jnp.sum((jnp.cumsum(onehot, axis=0) - 1) * onehot, axis=1)
    slot_index = owner_block * capacity + slot_rank
    groups = -(-capacity // LANES)
    group_id = owner_block * groups + slot_rank // LANES
    left = (group_id[:, None] == jnp.arange(row_count * groups, dtype=jnp.int32)[None, :]).astype(BF)
    lane = slot_rank % LANES
    hit = lane[:, None] == jnp.arange(LANES, dtype=jnp.int32)[None, :]
    high = jnp.where(hit, (offset // LANES)[:, None], 0).astype(BF)
    low = jnp.where(hit, (offset % LANES)[:, None], 0).astype(BF)
    high = lax.dot_general(left, high, (((0,), (0,)), ((), ())), preferred_element_type=F32)
    low = lax.dot_general(left, low, (((0,), (0,)), ((), ())), preferred_element_type=F32)
    requests = (high * LANES + low).astype(jnp.int32)
    requests = requests.reshape(row_count, groups * LANES)[:, :capacity]
    asked = lax.all_to_all(requests, "rows", split_axis=0, concat_axis=0, tiled=True)
    looked = table.at[asked.reshape(-1)].get(mode="promise_in_bounds")
    returned = lax.all_to_all(looked, "rows", split_axis=0, concat_axis=0, tiled=True)
    emb = returned.at[slot_index].get(mode="promise_in_bounds")
    emb = emb.reshape(batch_dev, full_len, col_width)
    return layer_call(
        col_count, lengths, emb, attn_gain, mlp_gain, w_qkv, w_out, w_in, w_down
    )


def solution(mesh):
    in_specs = (P("rows", "cols"), P("rows"), P("rows", "cols"), P(), P(), P(), P(), P(), P())
    out_specs = P("rows", "cols", None)
    return jax.shard_map(local, mesh=mesh, in_specs=in_specs, out_specs=out_specs, check_vma=False)
```

profile of v0, /device:TPU:26, one launch (start us, length us, event | category | flops | bytes accessed | tf_op | source)
XLA Modules:
  0.0 211.5 jit_solution(7588195970719247408)
XLA Ops:
  0.0 13.3 %all_gather.3 = s32[2,2048]{1,0:T(2,128)S(1)} all-gather(s32[2,512]{1,0:T(2,128)} %param.9), channel_id=1, replica_groups=mesh['rows'=8,'cols'=4] {'cols'}, dimensions={1}, use_global_device_ids=true | all-gather | bytes 20480 | tf_op jit(solution)/shard_map/all_gather | solution.py:213
  13.4 2.3 %reduce-window.6 = s32[8,32,128]{2,1,0:T(8,128)S(1)} reduce-window(s32[8,32,128]{2,1,0:T(8,128)S(1)} %fusion.15, s32[]{:T(128)} %constant.59.clone.1), window={size=1x1x128 pad=0_0x0_0x127_0}, to_apply=%region_0.1 | reduce-window | flops 4161536 | bytes 262148 | tf_op jit(solution)/shard_map/reduce-window
  15.7 0.3 slice_reduce_fusion
  16.0 0.2 reduce-window.9
  16.2 0.1 add_bitcast_fusion
  16.4 0.1 fusion.14
  16.5 2.4 %fusion.2 = f32[88,128]{1,0:T(8,128)S(1)} fusion(s32[4096]{0:T(1024)S(1)} %get-tuple-element.11, s32[4096]{0:T(1024)S(1)} %get-tuple-element.10, s32[4096]{0:T(1024)S(1)} %get-tuple-element.9), kind=kOutput, calls=%fused_computation.8 | convolution fusion | flops 94219264 | bytes 94208 | tf_op jit(solution)/shard_map/dot_general | solution.py:231
  19.0 2.4 %fusion.4 = s32[88,128]{1,0:T(8,128)S(1)} fusion(f32[88,128]{1,0:T(8,128)S(1)} %fusion.2, s32[4096]{0:T(1024)S(1)} %get-tuple-element.8, s32[4096]{0:T(1024)S(1)} %get-tuple-element.10, s32[4096]{0:T(1024)S(1)} %get-tuple-element.9), kind=kOutput, calls=%fused_computation.10 | convolution fusion | flops 94230528 | bytes 139264 | tf_op jit(solution)/shard_map/dot_general | solution.py:232
  21.4 7.5 %all_to_all.21 = s32[8,1,1376]{2,1,0:T(1,128)S(1)} all-to-all(s32[8,1,1376]{2,1,0:T(1,128)S(1)} %all_to_all.14), channel_id=1, replica_groups=mesh['rows'=8,'cols'=4] {'rows'}, dimensions={0} | all-to-all | bytes 88064 | tf_op jit(solution)/shard_map/all_to_all | solution.py:235
  28.9 0.1 reduce.1
  29.0 0.1 reshape.271
  29.2 0.1 fusion.16
  29.3 23.7 %gather_fusion = bf16[11008,128]{1,0:T(8,128)(2,1)} fusion(bf16[16384,128]{1,0:T(8,128)(2,1)} %param.11, s32[11264]{0:T(1024)S(1)} %pad_clamp_fusion), kind=kCustom, calls=%fused_computation | custom fusion | bytes 5680128 | tf_op jit(solution)/shard_map/gather | solution.py:236
  53.0 5.0 %all-to-all-start.1 = ((bf16[8,1376,128]{2,1,0:T(8,128)(2,1)}), bf16[8,1376,128]{2,1,0:T(8,128)(2,1)S(1)}, u32[]{:S(2)}, u32[]{:S(2)}) async-start(bf16[8,1376,128]{2,1,0:T(8,128)(2,1)} %bitcast.32), calls=%async_computation.1 | async-start | bytes 5636096 | tf_op jit(solution)/shard_map/all_to_all | solution.py:237
  58.1 2.4 %fusion.28 = (bf16[512,512]{1,0:T(8,128)(2,1)S(1)}, bf16[512,512]{1,0:T(8,128)(2,1)}, bf16[512,512]{1,0:T(8,128)(2,1)}) fusion(bf16[512,1536]{1,0:T(8,128)(2,1)} %param.13), kind=kLoop, calls=%fused_computation.70 | loop fusion | bytes 3145728 | tf_op jit(solution)/shard_map/slice | solution.py:176
  60.5 2.1 copy.16
  62.6 1.0 copy.17
  63.6 0.1 compare_select_fusion.1
  63.7 27.2 %all-to-all-done.1 = bf16[8,1376,128]{2,1,0:T(8,128)(2,1)S(1)} async-done(((bf16[8,1376,128]{2,1,0:T(8,128)(2,1)}), bf16[8,1376,128]{2,1,0:T(8,128)(2,1)S(1)}, u32[]{:S(2)}, u32[]{:S(2)}) %all-to-all-start.1) | async-done | bytes 2818080 | tf_op jit(solution)/shard_map/all_to_all | solution.py:237
  90.9 15.0 %gather_fusion.1 = bf16[4096,128]{1,0:T(8,128)(2,1)} fusion(bf16[11008,128]{1,0:T(8,128)(2,1)S(1)} %bitcast.31, s32[4096]{0:T(1024)S(1)} %broadcast_clamp_fusion), kind=kCustom, calls=%fused_computation.1 | custom fusion | bytes 2113536 | tf_op jit(solution)/shard_map/gather | solution.py:238
  105.9 103.4 %shard_map.91 = bf16[2,512,512]{2,1,0:T(8,128)(2,1)} custom-call(s32[2]{0:T(128)} %lens_ref.1, bf16[2,2048,128]{2,1,0:T(8,128)(2,1)} %bitcast.33, f32[1,512]{1,0:T(1,128)} %bitcast.45, f32[1,512]{1,0:T(1,128)} %bitcast.46, bf16[512,512]{1,0:T(8,128)(2,1)} %bitcast.34, bf16[512,512]{1,0:T(8,128)(2,1)} %get-tuple-element.7.wk_h, bf16[512,512]{1,0:T(8,128)(2,1)} %bitcast.35, ...), custom_call_target="tpu_custom_call" | custom-call | tf_op jit(solution)/shard_map/pallas_call | solution.py:182
  209.3 2.3 %copy.23 = bf16[2,512,512]{2,1,0:T(8,128)(2,1)} copy(bf16[2,512,512]{2,1,0:T(8,128)(2,1)} %shard_map.91) | data formatting | bytes 2097152
  (11 shorter events, 0.2 us)
Async XLA Ops:
  53.0 37.8 %all-to-all-start.1 = ((bf16[8,1376,128]{2,1,0:T(8,128)(2,1)}), bf16[8,1376,128]{2,1,0:T(8,128)(2,1)S(1)}, u32[]{:S(2)}, u32[]{:S(2)}) async-start(bf16[8,1376,128]{2,1,0:T(8,128)(2,1)} %bitcast.32), calls=%async_computation.1 | async-start | bytes 5636096 | tf_op jit(solution)/shard_map/all_to_all | solution.py:237
where the time goes:
time: 212 us
  Pallas kernels  103 us (49%)
  local copies, waits for them, and re-layouts  47 us (22%)
  waiting for transfers between devices  27.2 us (13%)
  blocking collectives  20.8 us (10%)
  starting transfers between devices  5 us (2%)
  matrix products  4.84 us (2%)
  other arithmetic  3.17 us (1%)
    pallas_call x1, Pallas kernels, layer_call(): pl.pallas_call(functools.partial(layer_kernel, cols), out_shape=jax.Shape...  103 us
    all_to_all x1, waiting for transfers between devices, local(): lax.all_to_all(looked, 'rows', split_axis=0, concat_axis=0, tiled=True)  27.2 us
    gather x1, local copies, waits for them, and re-layouts, local(): looked = table.at[asked.reshape(-1)].get(mode='promise_in_bounds')  23.7 us
    gather x1, local copies, waits for them, and re-layouts, local(): emb = returned.at[slot_index].get(mode='promise_in_bounds')  15 us
    all_gather x1, blocking collectives, local(): own_ids = lax.all_gather(token_ids, 'cols', axis=1, tiled=True)  13.3 us
    all_to_all x1, blocking collectives, local(): lax.all_to_all(requests, 'rows', split_axis=0, concat_axis=0, tiled=True)  7.5 us
    unnamed x5, local copies, waits for them, and re-layouts  5.36 us
    all_to_all x1, starting transfers between devices, local(): lax.all_to_all(looked, 'rows', split_axis=0, concat_axis=0, tiled=True)  5 us
  transfers between devices with their start and end apart: 1, of which 1 were waited for; matrix products, arithmetic and copies ran while one was open for 3% of the time, Pallas kernels for 0%

commit v1 on v0

v1 whole, which is shorter than its diff:
```python
import functools

import jax
import jax.numpy as jnp
from jax import lax
from jax.experimental import pallas as pl
from jax.experimental.pallas import tpu as pltpu
from jax.sharding import PartitionSpec as P

HEADS = 8
LANES = 128
NEG = -1e30
SCORE_SCALE = 0.125 * 1.4426950408889634
MESH = pl.DeviceIdType.MESH
BF = jnp.bfloat16
F32 = jnp.float32


def rms_norm(values_f32, gain):
    mean_sq = jnp.mean(values_f32 * values_f32, axis=-1, keepdims=True)
    return values_f32 * lax.rsqrt(mean_sq + 1e-06) * gain


def layer_kernel(
    cols, lens_ref, e_ref, gain1, gain2, wq_h, wk_h, wv_h, wo_h, wi_h, wd_h, out_ref,
    ebuf, hbuf, hstage, wq, wk, wv, wo, wi, wd, qm, k_s, v_s, m_s, l_s, acc,
    send_sem, pass_sem, recv_sem, hsend_sem, hrecv_sem, own_sem, w_sem,
):
    me = lax.axis_index("cols")
    batch, full, width = e_ref.shape
    quarter = full // cols
    half = quarter // 2
    head_dim = LANES // 2
    group = cols // batch
    hist = me // group
    other = batch - 1 - hist
    inner = group - 1 + hist
    far_inner = group - 1 + other
    mate = hist * group + (group - 1 - lax.rem(me, group))
    is_inner = me == inner
    lo = jnp.where(is_inner, 0, 1)
    hi = cols - 1 - lo
    mate_hi = cols - 2 + lo

    def chunk(j):
        return pl.ds(pl.multiple_of(j * quarter, quarter), quarter)

    def far_copy(j):
        return pltpu.make_async_remote_copy(
            src_ref=e_ref.at[other, chunk(j)],
            dst_ref=ebuf.at[me, j],
            send_sem=send_sem.at[0, j],
            recv_sem=recv_sem.at[me, j],
            device_id={"cols": far_inner},
            device_id_type=MESH,
        )

    def mate_copy(j):
        return pltpu.make_async_remote_copy(
            src_ref=e_ref.at[hist, chunk(j)],
            dst_ref=ebuf.at[me, j],
            send_sem=send_sem.at[1, j],
            recv_sem=recv_sem.at[me, j],
            device_id={"cols": mate},
            device_id_type=MESH,
        )

    def pass_copy(s, j):
        return pltpu.make_async_remote_copy(
            src_ref=ebuf.at[s, j],
            dst_ref=ebuf.at[s, j],
            send_sem=pass_sem.at[s, j],
            recv_sem=recv_sem.at[s, j],
            device_id={"cols": mate},
            device_id_type=MESH,
        )

    def own_copy(j):
        return pltpu.make_async_copy(e_ref.at[hist, chunk(j)], ebuf.at[me, j], own_sem.at[j])

    def hidden_copy(slot, q):
        return pltpu.make_async_remote_copy(
            src_ref=hstage.at[slot],
            dst_ref=hbuf.at[hist],
            send_sem=hsend_sem.at[slot],
            recv_sem=hrecv_sem.at[hist],
            device_id={"cols": q},
            device_id_type=MESH,
        )

    barrier = pltpu.get_barrier_semaphore()
    for off in range(1, cols):
        pl.semaphore_signal(
            barrier, inc=1, device_id={"cols": lax.rem(me + off, cols)}, device_id_type=MESH
        )
    pl.semaphore_wait(barrier, cols - 1)

    for j in reversed(range(cols)):
        far_copy(j).start()

        @pl.when(j <= mate_hi)
        def _():
            mate_copy(j).start()

        @pl.when(j <= hi)
        def _():
            own_copy(j).start()

    loads = [
        pltpu.make_async_copy(src, dst, w_sem.at[i])
        for i, (src, dst) in enumerate(
            ((wq_h, wq), (wk_h, wk), (wv_h, wv), (wo_h, wo), (wi_h, wi), (wd_h, wd))
        )
    ]
    for load in loads:
        load.start()
    for load in loads[:3]:
        load.wait()

    dims_nt = (((1,), (1,)), ((), ()))
    length = lens_ref[hist]

    def embedded(j):
        parts = [ebuf[s, j] for s in range(cols)]
        return jnp.concatenate(parts, axis=1).astype(F32)

    def flash(slot, h, k_blk, v_t, q0, qn, causal):
        s = jnp.dot(k_blk, qm[slot, h, :, q0 : q0 + qn], preferred_element_type=F32)
        kn = k_blk.shape[0]
        if causal:
            key_pos = lax.broadcasted_iota(jnp.int32, (kn, qn), 0)
            query_pos = lax.broadcasted_iota(jnp.int32, (kn, qn), 1) + q0
            s = jnp.where(key_pos <= query_pos, s, NEG)
        m_old = m_s[slot, h, :, q0 : q0 + qn]
        m_new = jnp.maximum(m_old, jnp.max(s, axis=0, keepdims=True))
        probs = jnp.exp2(s - m_new)
        alpha = jnp.exp2(m_old - m_new)
        m_s[slot, h, :, q0 : q0 + qn] = m_new
        l_s[slot, h, :, q0 : q0 + qn] = l_s[slot, h, :, q0 : q0 + qn] * alpha + jnp.sum(
            probs, axis=0, keepdims=True
        )
        acc[slot, h, :, q0 : q0 + qn] = acc[slot, h, :, q0 : q0 + qn] * alpha + jnp.dot(
            v_t, probs.astype(BF), preferred_element_type=F32
        )

    def attend(slot, causal):
        def pair(p, carry):
            for side in range(2):
                h = 2 * p + side
                wide = pl.ds(pl.multiple_of(p * 2 * LANES, 2 * LANES), 2 * LANES)
                rows = pl.ds(pl.multiple_of(h * head_dim, head_dim), head_dim)
                if causal:
                    flash(slot, h, k_s[:half, wide], v_s[rows, :half], 0, half, True)
                    flash(slot, h, k_s[:, wide], v_s[rows, :], half, half, True)
                else:
                    flash(slot, h, k_s[:, wide], v_s[rows, :], 0, quarter, False)
            return carry

        lax.fori_loop(0, HEADS // 2, pair, 0)

    def finish(slot, q):
        att_t = (acc[slot] / l_s[slot]).reshape(HEADS * head_dim, quarter)
        attended = att_t.T.astype(BF)
        hidden = embedded(q) + jnp.dot(attended, wo[...], preferred_element_type=F32)
        hstage[slot] = hidden.astype(BF)
        hidden_copy(slot, q).start()

    def key_step(i, carry):
        j = hi - i
        own_copy(j).wait()
        for s in range(cols):

            @pl.when(me != s)
            def _():
                pass_copy(s, j).wait_recv()

            @pl.when(is_inner & (s // group == other) & (j <= cols - 2))
            def _():
                pass_copy(s, j).start()

        normed = rms_norm(embedded(j), gain1[...]).astype(BF)
        keys = jnp.dot(normed, wk[...], preferred_element_type=F32).astype(BF)
        row = lax.broadcasted_iota(jnp.int32, (quarter, LANES), 0)
        lane = lax.broadcasted_iota(jnp.int32, (quarter, LANES), 1)
        dead = (lane == 0) & (row >= length - j * quarter)
        bias = jnp.where(dead, NEG, 0.0).astype(BF)
        for p in range(HEADS // 2):
            k_s[:, 2 * p * LANES : (2 * p + 1) * LANES] = keys[:, p * LANES : (p + 1) * LANES]
            k_s[:, (2 * p + 1) * LANES : (2 * p + 2) * LANES] = bias
        v_s[...] = lax.dot_general(wv[...], normed, dims_nt, preferred_element_type=F32).astype(BF)

        @pl.when((j == hi) | (j == lo))
        def _():
            slot = jnp.where(j == hi, 0, 1)
            q_t = lax.dot_general(wq[...], normed, dims_nt, preferred_element_type=F32)
            q_t = (q_t * SCORE_SCALE).astype(BF)
            zero = jnp.zeros((head_dim, quarter), BF)
            one_row = lax.broadcasted_iota(jnp.int32, (LANES, quarter), 0) == 0
            one_row = jnp.where(one_row, 1.0, 0.0).astype(BF)
            for h in range(HEADS):
                mine = q_t[h * head_dim : (h + 1) * head_dim]
                pair = (mine, zero) if h % 2 == 0 else (zero, mine)
                qm[slot, h] = jnp.concatenate(pair + (one_row,), axis=0)
            m_s[slot] = jnp.full(m_s.shape[1:], NEG, F32)
            l_s[slot] = jnp.zeros(l_s.shape[1:], F32)
            acc[slot] = jnp.zeros(acc.shape[1:], F32)

        def query_step(slot, carry):
            q = jnp.where(slot == 0, hi, lo)

            @pl.when(j == q)
            def _():
                attend(slot, True)

            @pl.when(j < q)
            def _():
                attend(slot, False)

            @pl.when(j == 0)
            def _():
                finish(slot, q)

            return carry

        lax.fori_loop(0, 2, query_step, 0)
        return carry

    loads[3].wait()
    lax.fori_loop(0, hi + 1, key_step, 0)
    loads[4].wait()
    loads[5].wait()

    def mlp(i, carry):
        h = jnp.where(i == 0, hist, other)
        pltpu.make_async_remote_copy(
            src_ref=hbuf.at[h],
            dst_ref=hbuf.at[h],
            send_sem=hsend_sem.at[0],
            recv_sem=hrecv_sem.at[h],
            device_id={"cols": mate},
            device_id_type=MESH,
        ).wait_recv()
        hidden = hbuf[h].astype(F32)
        normed_two = rms_norm(hidden, gain2[...]).astype(BF)
        ff = wd.shape[0]
        tile = 512
        total = hidden
        for f in range(0, ff, tile):
            gate = jnp.dot(normed_two, wi[:, f : f + tile], preferred_element_type=F32)
            up = jnp.dot(normed_two, wi[:, ff + f : ff + f + tile], preferred_element_type=F32)
            act = (gate / (1.0 + jnp.exp(-gate)) * up).astype(BF)
            total = total + jnp.dot(act, wd[f : f + tile, :], preferred_element_type=F32)
        out_ref[h] = total.astype(BF)
        return carry

    lax.fori_loop(0, batch, mlp, 0)
    for j in reversed(range(cols)):
        far_copy(j).wait_send()

        @pl.when(j <= mate_hi)
        def _():
            mate_copy(j).wait_send()

        for s in range(cols):

            @pl.when(is_inner & (s // group == other) & (j <= cols - 2))
            def _():
                pass_copy(s, j).wait_send()

    hidden_copy(0, hi).wait_send()
    hidden_copy(1, lo).wait_send()


def layer_call(cols, lengths, emb, gain1, gain2, w_qkv, w_out, w_in, w_down):
    batch, full, width = emb.shape
    assert batch == 2 and cols == 2 * batch
    quarter = full // cols
    d = width * cols
    wq_t = w_qkv[:, :d].T
    wk = w_qkv[:, d : 2 * d]
    wv_t = w_qkv[:, 2 * d :].T
    any_spec = pl.BlockSpec(memory_space=pl.ANY)
    vmem = pl.BlockSpec(memory_space=pltpu.VMEM)
    smem = pl.BlockSpec(memory_space=pltpu.SMEM)
    weights = (wq_t, wk, wv_t, w_out, w_in, w_down)
    head_dim = d // HEADS
    return pl.pallas_call(
        functools.partial(layer_kernel, cols),
        out_shape=jax.ShapeDtypeStruct((batch, quarter, d), BF),
        in_specs=[smem, any_spec, vmem, vmem] + [any_spec] * 6,
        out_specs=vmem,
        scratch_shapes=[
            pltpu.VMEM((cols, cols, quarter, width), BF),
            pltpu.VMEM((batch, quarter, d), BF),
            pltpu.VMEM((2, quarter, d), BF),
        ]
        + [pltpu.VMEM(w.shape, BF) for w in weights]
        + [
            pltpu.VMEM((2, HEADS, 4 * head_dim, quarter), BF),
            pltpu.VMEM((quarter, 2 * d), BF),
            pltpu.VMEM((d, quarter), BF),
            pltpu.VMEM((2, HEADS, 1, quarter), F32),
            pltpu.VMEM((2, HEADS, 1, quarter), F32),
            pltpu.VMEM((2, HEADS, head_dim, quarter), F32),
            pltpu.SemaphoreType.DMA((2, cols)),
            pltpu.SemaphoreType.DMA((cols, cols)),
            pltpu.SemaphoreType.DMA((cols, cols)),
            pltpu.SemaphoreType.DMA((2,)),
            pltpu.SemaphoreType.DMA((batch,)),
            pltpu.SemaphoreType.DMA((cols,)),
            pltpu.SemaphoreType.DMA((6,)),
        ],
        compiler_params=pltpu.CompilerParams(
            collective_id=0, has_side_effects=True, vmem_limit_bytes=60 * 1024 * 1024
        ),
    )(lengths, emb, gain1.reshape(1, d), gain2.reshape(1, d), *weights)


def local(token_ids, lengths, table, attn_gain, w_qkv, w_out, mlp_gain, w_in, w_down):
    batch_dev, quarter = token_ids.shape
    col_count = lax.axis_size("cols")
    row_count = lax.axis_size("rows")
    full_len = quarter * col_count
    block_rows, col_width = table.shape
    own_ids = lax.all_gather(token_ids, "cols", axis=1, tiled=True)
    flat_ids = own_ids.reshape(-1)
    token_count = flat_ids.shape[0]
    capacity = -(-(8 * token_count // (3 * row_count)) // 16) * 16
    owner_block = flat_ids // block_rows
    offset = flat_ids - owner_block * block_rows
    onehot = (owner_block[:, None] == jnp.arange(row_count, dtype=jnp.int32)[None, :]).astype(
        jnp.int32
    )
    slot_rank = jnp.sum((jnp.cumsum(onehot, axis=0) - 1) * onehot, axis=1)
    slot_index = owner_block * capacity + slot_rank
    groups = -(-capacity // LANES)
    group_id = owner_block * groups + slot_rank // LANES
    left = (group_id[:, None] == jnp.arange(row_count * groups, dtype=jnp.int32)[None, :]).astype(BF)
    lane = slot_rank % LANES
    hit = lane[:, None] == jnp.arange(LANES, dtype=jnp.int32)[None, :]
    high = jnp.where(hit, (offset // LANES)[:, None], 0).astype(BF)
    low = jnp.where(hit, (offset % LANES)[:, None], 0).astype(BF)
    high = lax.dot_general(left, high, (((0,), (0,)), ((), ())), preferred_element_type=F32)
    low = lax.dot_general(left, low, (((0,), (0,)), ((), ())), preferred_element_type=F32)
    requests = (high * LANES + low).astype(jnp.int32)
    requests = requests.reshape(row_count, groups * LANES)[:, :capacity]
    asked = lax.all_to_all(requests, "rows", split_axis=0, concat_axis=0, tiled=True)
    looked = table.at[asked.reshape(-1)].get(mode="promise_in_bounds")
    returned = lax.all_to_all(looked, "rows", split_axis=0, concat_axis=0, tiled=True)
    emb = returned.at[slot_index].get(mode="promise_in_bounds")
    emb = emb.reshape(batch_dev, full_len, col_width)
    return layer_call(
        col_count, lengths, emb, attn_gain, mlp_gain, w_qkv, w_out, w_in, w_down
    )


def solution(mesh):
    in_specs = (P("rows", "cols"), P("rows"), P("rows", "cols"), P(), P(), P(), P(), P(), P())
    out_specs = P("rows", "cols", None)
    return jax.shard_map(local, mesh=mesh, in_specs=in_specs, out_specs=out_specs, check_vma=False)
```

time: 212 us -> 191 us (0.901)
  the two profiles are of different devices: /device:TPU:26 before, /device:TPU:10 now
where the time goes in v1:
time: 191 us; the launch traced here: 190 us
  Pallas kernels  81.9 us (43%)
  local copies, waits for them, and re-layouts  47 us (25%)
  waiting for transfers between devices  27.2 us (14%)
  blocking collectives  21.1 us (11%)
  starting transfers between devices  5 us (3%)
  matrix products  4.84 us (3%)
  other arithmetic  3.17 us (2%)
    pallas_call x1, Pallas kernels, layer_call(): pl.pallas_call(functools.partial(layer_kernel, cols), out_shape=jax.Shape...  81.9 us
    all_to_all x1, waiting for transfers between devices, local(): lax.all_to_all(looked, 'rows', split_axis=0, concat_axis=0, tiled=True)  27.2 us
    gather x1, local copies, waits for them, and re-layouts, local(): looked = table.at[asked.reshape(-1)].get(mode='promise_in_bounds')  23.7 us
    gather x1, local copies, waits for them, and re-layouts, local(): emb = returned.at[slot_index].get(mode='promise_in_bounds')  15 us
    all_gather x1, blocking collectives, local(): own_ids = lax.all_gather(token_ids, 'cols', axis=1, tiled=True)  13.6 us
    all_to_all x1, blocking collectives, local(): lax.all_to_all(requests, 'rows', split_axis=0, concat_axis=0, tiled=True)  7.5 us
    unnamed x5, local copies, waits for them, and re-layouts  5.36 us
    all_to_all x1, starting transfers between devices, local(): lax.all_to_all(looked, 'rows', split_axis=0, concat_axis=0, tiled=True)  5 us
  transfers between devices with their start and end apart: 1, of which 1 were waited for; matrix products, arithmetic and copies ran while one was open for 3% of the time, Pallas kernels for 0%

profile of v1, /device:TPU:10, one launch (start us, length us, event | category | flops | bytes accessed | tf_op | source)
XLA Modules:
  0.0 190.3 jit_solution(7540168118756032284)
XLA Ops:
  0.0 13.6 %all_gather.3 = s32[2,2048]{1,0:T(2,128)S(1)} all-gather(s32[2,512]{1,0:T(2,128)} %param.9), channel_id=1, replica_groups=mesh['rows'=8,'cols'=4] {'cols'}, dimensions={1}, use_global_device_ids=true | all-gather | bytes 20480 | tf_op jit(solution)/shard_map/all_gather | solution.py:325
  13.6 2.3 %reduce-window.6 = s32[8,32,128]{2,1,0:T(8,128)S(1)} reduce-window(s32[8,32,128]{2,1,0:T(8,128)S(1)} %fusion.15, s32[]{:T(128)} %constant.59.clone.1), window={size=1x1x128 pad=0_0x0_0x127_0}, to_apply=%region_0.1 | reduce-window | flops 4161536 | bytes 262148 | tf_op jit(solution)/shard_map/reduce-window
  15.9 0.3 slice_reduce_fusion
  16.2 0.2 reduce-window.9
  16.4 0.1 add_bitcast_fusion
  16.6 0.1 fusion.14
  16.8 2.4 %fusion.2 = f32[88,128]{1,0:T(8,128)S(1)} fusion(s32[4096]{0:T(1024)S(1)} %get-tuple-element.11, s32[4096]{0:T(1024)S(1)} %get-tuple-element.10, s32[4096]{0:T(1024)S(1)} %get-tuple-element.9), kind=kOutput, calls=%fused_computation.8 | convolution fusion | flops 94219264 | bytes 94208 | tf_op jit(solution)/shard_map/dot_general | solution.py:343
  19.2 2.4 %fusion.4 = s32[88,128]{1,0:T(8,128)S(1)} fusion(f32[88,128]{1,0:T(8,128)S(1)} %fusion.2, s32[4096]{0:T(1024)S(1)} %get-tuple-element.8, s32[4096]{0:T(1024)S(1)} %get-tuple-element.10, s32[4096]{0:T(1024)S(1)} %get-tuple-element.9), kind=kOutput, calls=%fused_computation.10 | convolution fusion | flops 94230528 | bytes 139264 | tf_op jit(solution)/shard_map/dot_general | solution.py:344
  21.7 7.5 %all_to_all.21 = s32[8,1,1376]{2,1,0:T(1,128)S(1)} all-to-all(s32[8,1,1376]{2,1,0:T(1,128)S(1)} %all_to_all.14), channel_id=1, replica_groups=mesh['rows'=8,'cols'=4] {'rows'}, dimensions={0} | all-to-all | bytes 88064 | tf_op jit(solution)/shard_map/all_to_all | solution.py:347
  29.2 0.1 reduce.1
  29.3 0.1 reshape.271
  29.4 0.1 fusion.16
  29.6 23.7 %gather_fusion = bf16[11008,128]{1,0:T(8,128)(2,1)} fusion(bf16[16384,128]{1,0:T(8,128)(2,1)} %param.11, s32[11264]{0:T(1024)S(1)} %pad_clamp_fusion), kind=kCustom, calls=%fused_computation | custom fusion | bytes 5680128 | tf_op jit(solution)/shard_map/gather | solution.py:348
  53.3 5.0 %all-to-all-start.1 = ((bf16[8,1376,128]{2,1,0:T(8,128)(2,1)}), bf16[8,1376,128]{2,1,0:T(8,128)(2,1)S(1)}, u32[]{:S(2)}, u32[]{:S(2)}) async-start(bf16[8,1376,128]{2,1,0:T(8,128)(2,1)} %bitcast.32), calls=%async_computation.1 | async-start | bytes 5636096 | tf_op jit(solution)/shard_map/all_to_all | solution.py:349
  58.3 2.4 %fusion.28 = (bf16[512,512]{1,0:T(8,128)(2,1)S(1)}, bf16[512,512]{1,0:T(8,128)(2,1)}, bf16[512,512]{1,0:T(8,128)(2,1)}) fusion(bf16[512,1536]{1,0:T(8,128)(2,1)} %param.13), kind=kLoop, calls=%fused_computation.70 | loop fusion | bytes 3145728 | tf_op jit(solution)/shard_map/slice | solution.py:281
  60.7 2.1 %copy.16 = bf16[512,512]{0,1:T(8,128)(2,1)} copy(bf16[512,512]{1,0:T(8,128)(2,1)} %get-tuple-element.6) | data formatting | bytes 1048576
  62.8 1.0 copy.17
  63.8 0.1 compare_select_fusion.1
  63.9 27.2 %all-to-all-done.1 = bf16[8,1376,128]{2,1,0:T(8,128)(2,1)S(1)} async-done(((bf16[8,1376,128]{2,1,0:T(8,128)(2,1)}), bf16[8,1376,128]{2,1,0:T(8,128)(2,1)S(1)}, u32[]{:S(2)}, u32[]{:S(2)}) %all-to-all-start.1) | async-done | bytes 2818080 | tf_op jit(solution)/shard_map/all_to_all | solution.py:349
  91.1 15.0 %gather_fusion.1 = bf16[4096,128]{1,0:T(8,128)(2,1)} fusion(bf16[11008,128]{1,0:T(8,128)(2,1)S(1)} %bitcast.31, s32[4096]{0:T(1024)S(1)} %broadcast_clamp_fusion), kind=kCustom, calls=%fused_computation.1 | custom fusion | bytes 2113536 | tf_op jit(solution)/shard_map/gather | solution.py:350
  106.1 81.9 %shard_map.91 = bf16[2,512,512]{2,1,0:T(8,128)(2,1)} custom-call(s32[2]{0:T(128)} %lens_ref.1, bf16[2,2048,128]{2,1,0:T(8,128)(2,1)} %bitcast.33, f32[1,512]{1,0:T(1,128)} %bitcast.45, f32[1,512]{1,0:T(1,128)} %bitcast.46, bf16[512,512]{1,0:T(8,128)(2,1)} %bitcast.34, bf16[512,512]{1,0:T(8,128)(2,1)} %get-tuple-element.7.wk_h, bf16[512,512]{1,0:T(8,128)(2,1)} %bitcast.35, ...), custom_call_target="tpu_custom_call" | custom-call | tf_op jit(solution)/shard_map/pallas_call | solution.py:287
  188.0 2.3 %copy.23 = bf16[2,512,512]{2,1,0:T(8,128)(2,1)} copy(bf16[2,512,512]{2,1,0:T(8,128)(2,1)} %shard_map.91) | data formatting | bytes 2097152
  (11 shorter events, 0.2 us)
Async XLA Ops:
  53.3 37.9 %all-to-all-start.1 = ((bf16[8,1376,128]{2,1,0:T(8,128)(2,1)}), bf16[8,1376,128]{2,1,0:T(8,128)(2,1)S(1)}, u32[]{:S(2)}, u32[]{:S(2)}) async-start(bf16[8,1376,128]{2,1,0:T(8,128)(2,1)} %bitcast.32), calls=%async_computation.1 | async-start | bytes 5636096 | tf_op jit(solution)/shard_map/all_to_all | solution.py:349

commit v2 on v1

--- a/solution.py
+++ b/solution.py
@@ -316,39 +316,272 @@
     )(lengths, emb, gain1.reshape(1, d), gain2.reshape(1, d), *weights)
 
 
+def fetch_kernel(
+    rows, cols, cap, ids_ref, table_ref, ret_ref, slot_ref,
+    ids_all, ids_s, left, right, req, asked, asked_s, tab, wide_tab, stage, outbox,
+    ids_send, ids_recv, req_send, req_recv, row_send, row_recv, tab_sem, smem_sem, own_sem,
+):
+    mc = lax.axis_index("cols")
+    mr = lax.axis_index("rows")
+    batch, quarter = ids_ref.shape
+    block_rows, width = table_ref.shape
+    tiles = quarter // LANES
+    lines = ids_s.shape[0]
+    tokens = lines * LANES
+    groups = req.shape[1]
+    pieces = tab_sem.shape[0]
+    piece = block_rows // pieces
+    shift = block_rows.bit_length() - 1
+
+    def tab_copy(i):
+        part = pl.ds(i * piece, piece)
+        return pltpu.make_async_copy(table_ref.at[part], tab.at[part], tab_sem.at[i])
+
+    for i in range(pieces):
+        tab_copy(i).start()
+
+    def ids_copy(c):
+        return pltpu.make_async_remote_copy(
+            src_ref=ids_ref,
+            dst_ref=ids_all.at[mc],
+            send_sem=ids_send.at[c],
+            recv_sem=ids_recv.at[mc],
+            device_id={"cols": c},
+            device_id_type=MESH,
+        )
+
+    def ids_arrival(c):
+        return pltpu.make_async_remote_copy(
+            src_ref=ids_ref,
+            dst_ref=ids_all.at[c],
+            send_sem=ids_send.at[c],
+            recv_sem=ids_recv.at[c],
+            device_id={"cols": c},
+            device_id_type=MESH,
+        )
+
+    def req_copy(r):
+        return pltpu.make_async_remote_copy(
+            src_ref=req.at[r],
+            dst_ref=asked.at[mr],
+            send_sem=req_send.at[r],
+            recv_sem=req_recv.at[mr],
+            device_id={"rows": r},
+            device_id_type=MESH,
+        )
+
+    def req_arrival(r):
+        return pltpu.make_async_remote_copy(
+            src_ref=req.at[r],
+            dst_ref=asked.at[r],
+            send_sem=req_send.at[r],
+            recv_sem=req_recv.at[r],
+            device_id={"rows": r},
+            device_id_type=MESH,
+        )
+
+    def row_copy(r):
+        return pltpu.make_async_remote_copy(
+            src_ref=outbox.at[r],
+            dst_ref=ret_ref.at[mr],
+            send_sem=row_send.at[r],
+            recv_sem=row_recv.at[mr],
+            device_id={"rows": r},
+            device_id_type=MESH,
+        )
+
+    def row_arrival(r):
+        return pltpu.make_async_remote_copy(
+            src_ref=outbox.at[r],
+            dst_ref=ret_ref.at[r],
+            send_sem=row_send.at[r],
+            recv_sem=row_recv.at[r],
+            device_id={"rows": r},
+            device_id_type=MESH,
+        )
+
+    barrier = pltpu.get_barrier_semaphore()
+    for off in range(1, cols):
+        pl.semaphore_signal(
+            barrier, inc=1, device_id={"cols": lax.rem(mc + off, cols)}, device_id_type=MESH
+        )
+    for off in range(1, rows):
+        pl.semaphore_signal(
+            barrier, inc=1, device_id={"rows": lax.rem(mr + off, rows)}, device_id_type=MESH
+        )
+    pl.semaphore_wait(barrier, cols - 1 + rows - 1)
+
+    for off in range(1, cols):
+        ids_copy(lax.rem(mc + off, cols)).start()
+    ids_all[mc] = ids_ref[...]
+
+    step = 512
+    for i in range(pieces):
+        tab_copy(i).wait()
+
+        def widen(k, carry):
+            part = pl.ds(pl.multiple_of(i * piece + k * step, step), step)
+            wide_tab[part, :] = tab[part, :].astype(F32)
+            return carry
+
+        lax.fori_loop(0, piece // step, widen, 0)
+
+    for off in range(1, cols):
+        ids_arrival(lax.rem(mc + off, cols)).wait_recv()
+    for c in range(cols):
+        for b in range(batch):
+            for k in range(tiles):
+                line = (c * batch + b) * tiles + k
+                ids_s[line : line + 1, :] = ids_all[c, b : b + 1, k * LANES : (k + 1) * LANES]
+    ids = ids_s[...]
+    owner = lax.shift_right_logical(ids, shift)
+    offset = ids - owner * block_rows
+
+    src_lane = lax.broadcasted_iota(jnp.int32, (LANES, 2 * LANES), 0)
+    dst_lane = lax.broadcasted_iota(jnp.int32, (LANES, 2 * LANES), 1)
+    before = jnp.where(src_lane < dst_lane, 1.0, 0.0).astype(BF)
+    line_a = lax.broadcasted_iota(jnp.int32, (lines, lines), 0)
+    line_b = lax.broadcasted_iota(jnp.int32, (lines, lines), 1)
+    above = jnp.where(line_b < line_a, 1.0, 0.0).astype(BF)
+    rank = jnp.zeros((lines, LANES), F32)
+    for r in range(rows):
+        mine = owner == r
+        counts = jnp.dot(
+            jnp.where(mine, 1.0, 0.0).astype(BF), before, preferred_element_type=F32
+        )
+        earlier = jnp.dot(above, counts[:, LANES:].astype(BF), preferred_element_type=F32)
+        rank = rank + jnp.where(mine, counts[:, :LANES] + earlier, 0.0)
+    rank = rank.astype(jnp.int32)
+    slot_ref[...] = owner * cap + rank
+    group = owner * groups + lax.shift_right_logical(rank, 7)
+    lane = rank - lax.shift_right_logical(rank, 7) * LANES
+    high = lax.shift_right_logical(offset, 7)
+    low = (offset - high * LANES).astype(F32)
+    high = high.astype(F32)
+    group_iota = lax.broadcasted_iota(jnp.int32, (rows * groups, LANES), 0)
+    lane_iota = lax.broadcasted_iota(jnp.int32, (LANES, LANES), 0)
+    for k in range(lines):
+        part = slice(k * LANES, (k + 1) * LANES)
+        line = slice(k, k + 1)
+        left[:, part] = jnp.where(group[line] == group_iota, 1.0, 0.0).astype(BF)
+        hit = lane[line] == lane_iota
+        right[:LANES, part] = jnp.where(hit, high[line], 0.0).astype(BF)
+        right[LANES:, part] = jnp.where(hit, low[line], 0.0).astype(BF)
+    found = lax.dot_general(
+        left[...], right[...], (((1,), (1,)), ((), ())), preferred_element_type=F32
+    )
+    found = (found[:, :LANES] * LANES + found[:, LANES:]).astype(jnp.int32)
+    found = jnp.minimum(jnp.maximum(found, 0), block_rows - 1)
+    req[...] = found.reshape(rows, groups, LANES)
+
+    def over_rows(act):
+        def body(i, carry):
+            act(lax.rem(mr + i + 1, rows))
+            return carry
+
+        lax.fori_loop(0, rows - 1, body, 0)
+
+    over_rows(lambda r: req_copy(r).start())
+    asked[mr] = req[mr]
+    over_rows(lambda r: req_arrival(r).wait_recv())
+    to_smem = pltpu.make_async_copy(asked, asked_s, smem_sem)
+    to_smem.start()
+    to_smem.wait()
+
+    unroll = stage.shape[0]
+    own = pltpu.make_async_copy(outbox.at[mr], ret_ref.at[mr], own_sem)
+
+    def serve(i, carry):
+        dist = (i + 1) // 2
+        off = rows // 2 + dist * (1 - 2 * lax.rem(i, 2))
+        r = lax.rem(mr + off, rows)
+
+        def some(k, carry):
+            base = k * unroll
+            g = base // LANES
+            first = base - g * LANES
+            for u in range(unroll):
+                at = asked_s[r, g, first + u]
+                stage[u : u + 1, :] = wide_tab[pl.ds(at, 1), :]
+            outbox[r, pl.ds(pl.multiple_of(base, unroll), unroll), :] = stage[...].astype(BF)
+            return carry
+
+        lax.fori_loop(0, cap // unroll, some, 0)
+
+        @pl.when(i < rows - 1)
+        def _():
+            row_copy(r).start()
+
+        return carry
+
+    lax.fori_loop(0, rows, serve, 0)
+    own.start()
+    own.wait()
+    over_rows(lambda r: row_arrival(r).wait_recv())
+    for off in range(1, cols):
+        ids_copy(lax.rem(mc + off, cols)).wait_send()
+    over_rows(lambda r: req_copy(r).wait_send())
+    over_rows(lambda r: row_copy(r).wait_send())
+
+
+def fetch_call(rows, cols, cap, token_ids, table):
+    batch, quarter = token_ids.shape
+    tokens = batch * quarter * cols
+    lines = tokens // LANES
+    block_rows, width = table.shape
+    assert block_rows & (block_rows - 1) == 0 and rows % 2 == 0
+    groups = -(-cap // (8 * LANES)) * 8
+    any_spec = pl.BlockSpec(memory_space=pl.ANY)
+    vmem = pl.BlockSpec(memory_space=pltpu.VMEM)
+    dma = pltpu.SemaphoreType.DMA
+    return pl.pallas_call(
+        functools.partial(fetch_kernel, rows, cols, cap),
+        out_shape=(
+            jax.ShapeDtypeStruct((rows, cap, width), BF),
+            jax.ShapeDtypeStruct((lines, LANES), jnp.int32),
+        ),
+        in_specs=[vmem, any_spec],
+        out_specs=(any_spec, vmem),
+        scratch_shapes=[
+            pltpu.VMEM((cols, batch, quarter), jnp.int32),
+            pltpu.VMEM((lines, LANES), jnp.int32),
+            pltpu.VMEM((rows * groups, tokens), BF),
+            pltpu.VMEM((2 * LANES, tokens), BF),
+            pltpu.VMEM((rows, groups, LANES), jnp.int32),
+            pltpu.VMEM((rows, groups, LANES), jnp.int32),
+            pltpu.SMEM((rows, groups, LANES), jnp.int32),
+            pltpu.VMEM((block_rows, width), BF),
+            pltpu.VMEM((block_rows, width), F32),
+            pltpu.VMEM((32, width), F32),
+            pltpu.VMEM((rows, cap, width), BF),
+            dma((cols,)),
+            dma((cols,)),
+            dma((rows,)),
+            dma((rows,)),
+            dma((rows,)),
+            dma((rows,)),
+            dma((4,)),
+            dma,
+            dma,
+        ],
+        compiler_params=pltpu.CompilerParams(
+            collective_id=1, has_side_effects=True, vmem_limit_bytes=60 * 1024 * 1024
+        ),
+    )(token_ids, table)
+
+
 def local(token_ids, lengths, table, attn_gain, w_qkv, w_out, mlp_gain, w_in, w_down):
     batch_dev, quarter = token_ids.shape
     col_count = lax.axis_size("cols")
     row_count = lax.axis_size("rows")
     full_len = quarter * col_count
-    block_rows, col_width = table.shape
-    own_ids = lax.all_gather(token_ids, "cols", axis=1, tiled=True)
-    flat_ids = own_ids.reshape(-1)
-    token_count = flat_ids.shape[0]
-    capacity = -(-(8 * token_count // (3 * row_count)) // 16) * 16
-    owner_block = flat_ids // block_rows
-    offset = flat_ids - owner_block * block_rows
-    onehot = (owner_block[:, None] == jnp.arange(row_count, dtype=jnp.int32)[None, :]).astype(
-        jnp.int32
-    )
-    slot_rank = jnp.sum((jnp.cumsum(onehot, axis=0) - 1) * onehot, axis=1)
-    slot_index = owner_block * capacity + slot_rank
-    groups = -(-capacity // LANES)
-    group_id = owner_block * groups + slot_rank // LANES
-    left = (group_id[:, None] == jnp.arange(row_count * groups, dtype=jnp.int32)[None, :]).astype(BF)
-    lane = slot_rank % LANES
-    hit = lane[:, None] == jnp.arange(LANES, dtype=jnp.int32)[None, :]
-    high = jnp.where(hit, (offset // LANES)[:, None], 0).astype(BF)
-    low = jnp.where(hit, (offset % LANES)[:, None], 0).astype(BF)
-    high = lax.dot_general(left, high, (((0,), (0,)), ((), ())), preferred_element_type=F32)
-    low = lax.dot_general(left, low, (((0,), (0,)), ((), ())), preferred_element_type=F32)
-    requests = (high * LANES + low).astype(jnp.int32)
-    requests = requests.reshape(row_count, groups * LANES)[:, :capacity]
-    asked = lax.all_to_all(requests, "rows", split_axis=0, concat_axis=0, tiled=True)
-    looked = table.at[asked.reshape(-1)].get(mode="promise_in_bounds")
-    returned = lax.all_to_all(looked, "rows", split_axis=0, concat_axis=0, tiled=True)
-    emb = returned.at[slot_index].get(mode="promise_in_bounds")
-    emb = emb.reshape(batch_dev, full_len, col_width)
+    token_count = batch_dev * full_len
+    capacity = -(-(8 * token_count // (3 * row_count)) // 32) * 32
+    returned, slots = fetch_call(row_count, col_count, capacity, token_ids, table)
+    slots = slots.reshape(col_count, batch_dev, quarter).transpose(1, 0, 2).reshape(-1)
+    flat = returned.reshape(row_count * capacity, -1)
+    emb = flat.at[slots].get(mode="promise_in_bounds")
+    emb = emb.reshape(batch_dev, full_len, -1)
     return layer_call(
         col_count, lengths, emb, attn_gain, mlp_gain, w_qkv, w_out, w_in, w_down
     )

time: 191 us -> 162 us (0.85)
  the two profiles are of different devices: /device:TPU:10 before, /device:TPU:14 now
where the time goes in v2:
time: 162 us
  Pallas kernels  139 us (86%)
  local copies, waits for them, and re-layouts  22.6 us (14%)
    pallas_call x1, Pallas kernels, layer_call(): pl.pallas_call(functools.partial(layer_kernel, cols), out_shape=jax.Shape...  84.3 us
    pallas_call x1, Pallas kernels, fetch_call(): pl.pallas_call(functools.partial(fetch_kernel, rows, cols, cap), out_shap...  54.7 us
    gather x1, local copies, waits for them, and re-layouts, local(): emb = flat.at[slots].get(mode='promise_in_bounds')  16.6 us
    unnamed x5, local copies, waits for them, and re-layouts  4.28 us

profile of v2, /device:TPU:14, one launch (start us, length us, event | category | flops | bytes accessed | tf_op | source)
XLA Modules:
  0.0 161.7 jit_solution(10349092767808098294)
XLA Ops:
  0.0 54.7 %shard_map.91 = (bf16[8,1376,128]{2,1,0:T(8,128)(2,1)}, s32[32,128]{1,0:T(8,128)}) custom-call(s32[2,512]{1,0:T(2,128)} %ids_ref.1, bf16[16384,128]{1,0:T(8,128)(2,1)} %table_ref.1), custom_call_target="tpu_custom_call" | custom-call | tf_op jit(solution)/shard_map/pallas_call | solution.py:537
  54.7 0.7 reshape.47
  55.5 0.0 copy-start
  55.5 16.6 %gather_fusion = bf16[4096,128]{1,0:T(8,128)(2,1)} fusion(bf16[11008,128]{1,0:T(8,128)(2,1)} %bitcast.10, s32[4096]{0:T(1024)S(1)} %broadcast_clamp_fusion), kind=kCustom, calls=%fused_computation | custom fusion | bytes 2113536 | tf_op jit(solution)/shard_map/gather | solution.py:583
  72.2 0.0 copy-done
  72.2 0.9 fusion
  73.1 1.0 copy.15
  74.1 1.0 copy.16
  75.1 84.3 %shard_map.92 = bf16[2,512,512]{2,1,0:T(8,128)(2,1)} custom-call(s32[2]{0:T(128)} %lens_ref.1, bf16[2,2048,128]{2,1,0:T(8,128)(2,1)} %bitcast.11, f32[1,512]{1,0:T(1,128)} %bitcast.16, f32[1,512]{1,0:T(1,128)} %bitcast.17, bf16[512,512]{1,0:T(8,128)(2,1)} %bitcast.12, bf16[512,512]{1,0:T(8,128)(2,1)} %get-tuple-element.11.wk_h, bf16[512,512]{1,0:T(8,128)(2,1)} %bitcast.13, ...), custom_call_target="tpu_custom_call" | custom-call | tf_op jit(solution)/shard_map/pallas_call | solution.py:287
  159.4 2.3 %copy.20 = bf16[2,512,512]{2,1,0:T(8,128)(2,1)} copy(bf16[2,512,512]{2,1,0:T(8,128)(2,1)} %shard_map.92) | data formatting | bytes 2097152
  (4 shorter events, 0.1 us)
Async XLA Ops:
  55.5 16.7 %copy-start = (bf16[512,1536]{1,0:T(8,128)(2,1)S(1)}, bf16[512,1536]{1,0:T(8,128)(2,1)}, u32[]{:S(2)}) copy-start(bf16[512,1536]{1,0:T(8,128)(2,1)} %param.13) | copy-start | bytes 4718596

commit v3 on v2

--- a/solution.py
+++ b/solution.py
@@ -22,13 +22,13 @@
 
 
 def layer_kernel(
-    cols, lens_ref, e_ref, gain1, gain2, wq_h, wk_h, wv_h, wo_h, wi_h, wd_h, out_ref,
-    ebuf, hbuf, hstage, wq, wk, wv, wo, wi, wd, qm, k_s, v_s, m_s, l_s, acc,
-    send_sem, pass_sem, recv_sem, hsend_sem, hrecv_sem, own_sem, w_sem,
+    cols, batch, lens_ref, slots_ref, raw_ref, gain1, gain2, wq_h, wk_h, wv_h, wo_h, wi_h, wd_h,
+    out_ref, raw, wide, stage, ebox, ebuf, hbuf, hstage, wq, wk, wv, wo, wi, wd, qm, k_s, v_s,
+    m_s, l_s, acc, raw_sem, send_sem, pass_sem, recv_sem, hsend_sem, hrecv_sem, w_sem,
 ):
     me = lax.axis_index("cols")
-    batch, full, width = e_ref.shape
-    quarter = full // cols
+    rows, cap, width = raw_ref.shape
+    quarter = ebox.shape[1]
     half = quarter // 2
     head_dim = LANES // 2
     group = cols // batch
@@ -38,16 +38,23 @@
     far_inner = group - 1 + other
     mate = hist * group + (group - 1 - lax.rem(me, group))
     is_inner = me == inner
-    lo = jnp.where(is_inner, 0, 1)
-    hi = cols - 1 - lo
-    mate_hi = cols - 2 + lo
-
-    def chunk(j):
-        return pl.ds(pl.multiple_of(j * quarter, quarter), quarter)
+    falling = hist == 0
+    hi = jnp.where(is_inner, cols - 2, cols - 1)
+    mate_hi = jnp.where(is_inner, cols - 1, cols - 2)
+    q_sent = jnp.where(falling, hi, cols - 1 - hi)
+    q_kept = cols - 1 - q_sent
+
+    def order(h, t):
+        return jnp.where(h == 0, cols - 1 - t, t)
+
+    def raw_copy(r):
+        return pltpu.make_async_copy(
+            raw_ref.at[r], raw.at[pl.ds(pl.multiple_of(r * cap, 16), cap)], raw_sem.at[r]
+        )
 
     def far_copy(j):
         return pltpu.make_async_remote_copy(
-            src_ref=e_ref.at[other, chunk(j)],
+            src_ref=ebox.at[j],
             dst_ref=ebuf.at[me, j],
             send_sem=send_sem.at[0, j],
             recv_sem=recv_sem.at[me, j],
@@ -57,7 +64,7 @@
 
     def mate_copy(j):
         return pltpu.make_async_remote_copy(
-            src_ref=e_ref.at[hist, chunk(j)],
+            src_ref=ebuf.at[me, j],
             dst_ref=ebuf.at[me, j],
             send_sem=send_sem.at[1, j],
             recv_sem=recv_sem.at[me, j],
@@ -75,46 +82,72 @@
             device_id_type=MESH,
         )
 
-    def own_copy(j):
-        return pltpu.make_async_copy(e_ref.at[hist, chunk(j)], ebuf.at[me, j], own_sem.at[j])
-
-    def hidden_copy(slot, q):
-        return pltpu.make_async_remote_copy(
-            src_ref=hstage.at[slot],
+    def hidden_copy():
+        return pltpu.make_async_remote_copy(
+            src_ref=hstage,
             dst_ref=hbuf.at[hist],
-            send_sem=hsend_sem.at[slot],
-            recv_sem=hrecv_sem.at[hist],
-            device_id={"cols": q},
-            device_id_type=MESH,
-        )
+            send_sem=hsend_sem,
+            recv_sem=hrecv_sem,
+            device_id={"cols": q_sent},
+            device_id_type=MESH,
+        )
+
+    def start_raw(r, carry):
+        raw_copy(r).start()
+        return carry
+
+    lax.fori_loop(0, rows, start_raw, 0)
+    loads = [
+        pltpu.make_async_copy(src, dst, w_sem.at[i])
+        for i, (src, dst) in enumerate(
+            ((wq_h, wq), (wk_h, wk), (wv_h, wv), (wo_h, wo), (wi_h, wi), (wd_h, wd))
+        )
+    ]
+    for load in loads:
+        load.start()
 
     barrier = pltpu.get_barrier_semaphore()
     for off in range(1, cols):
         pl.semaphore_signal(
             barrier, inc=1, device_id={"cols": lax.rem(me + off, cols)}, device_id_type=MESH
         )
+
+    def widen(r, carry):
+        raw_copy(r).wait()
+        part = pl.ds(pl.multiple_of(r * cap, 16), cap)
+        wide[part, :] = raw[part, :].astype(F32)
+        return carry
+
+    lax.fori_loop(0, rows, widen, 0)
     pl.semaphore_wait(barrier, cols - 1)
 
-    for j in reversed(range(cols)):
-        far_copy(j).start()
-
-        @pl.when(j <= mate_hi)
-        def _():
-            mate_copy(j).start()
-
-        @pl.when(j <= hi)
-        def _():
-            own_copy(j).start()
-
-    loads = [
-        pltpu.make_async_copy(src, dst, w_sem.at[i])
-        for i, (src, dst) in enumerate(
-            ((wq_h, wq), (wk_h, wk), (wv_h, wv), (wo_h, wo), (wi_h, wi), (wd_h, wd))
-        )
-    ]
+    tiles = quarter // LANES
+
+    def pick(t, carry):
+        for side in range(2):
+            h = other if side == 0 else hist
+            j = order(h, t)
+            line = (j * batch + h) * tiles
+            for k in range(tiles):
+                for u in range(LANES):
+                    stage[u : u + 1, :] = wide[pl.ds(slots_ref[line + k, u], 1), :]
+                part = slice(k * LANES, (k + 1) * LANES)
+                if side == 0:
+                    ebox[j, part, :] = stage[...].astype(BF)
+                else:
+                    ebuf[me, j, part, :] = stage[...].astype(BF)
+            if side == 0:
+                far_copy(j).start()
+            else:
+
+                @pl.when(j <= mate_hi)
+                def _():
+                    mate_copy(j).start()
+
+        return carry
+
+    lax.fori_loop(0, cols, pick, 0)
     for load in loads:
-        load.start()
-    for load in loads[:3]:
         load.wait()
 
     dims_nt = (((1,), (1,)), ((), ()))
@@ -143,41 +176,34 @@
             v_t, probs.astype(BF), preferred_element_type=F32
         )
 
-    def attend(slot, causal):
+    def attend(slot, j, causal):
         def pair(p, carry):
             for side in range(2):
                 h = 2 * p + side
-                wide = pl.ds(pl.multiple_of(p * 2 * LANES, 2 * LANES), 2 * LANES)
-                rows = pl.ds(pl.multiple_of(h * head_dim, head_dim), head_dim)
+                wide_p = pl.ds(pl.multiple_of(p * 2 * LANES, 2 * LANES), 2 * LANES)
+                part = pl.ds(pl.multiple_of(h * head_dim, head_dim), head_dim)
                 if causal:
-                    flash(slot, h, k_s[:half, wide], v_s[rows, :half], 0, half, True)
-                    flash(slot, h, k_s[:, wide], v_s[rows, :], half, half, True)
+                    flash(slot, h, k_s[j, :half, wide_p], v_s[j, part, :half], 0, half, True)
+                    flash(slot, h, k_s[j, :, wide_p], v_s[j, part, :], half, half, True)
                 else:
-                    flash(slot, h, k_s[:, wide], v_s[rows, :], 0, quarter, False)
+                    flash(slot, h, k_s[j, :, wide_p], v_s[j, part, :], 0, quarter, False)
             return carry
 
         lax.fori_loop(0, HEADS // 2, pair, 0)
 
-    def finish(slot, q):
-        att_t = (acc[slot] / l_s[slot]).reshape(HEADS * head_dim, quarter)
-        attended = att_t.T.astype(BF)
-        hidden = embedded(q) + jnp.dot(attended, wo[...], preferred_element_type=F32)
-        hstage[slot] = hidden.astype(BF)
-        hidden_copy(slot, q).start()
-
-    def key_step(i, carry):
-        j = hi - i
-        own_copy(j).wait()
+    def arrive(j):
         for s in range(cols):
-
-            @pl.when(me != s)
+            far = s // group == other
+
+            @pl.when(far | ((s != me) & (j <= hi)))
             def _():
                 pass_copy(s, j).wait_recv()
 
-            @pl.when(is_inner & (s // group == other) & (j <= cols - 2))
+            @pl.when(is_inner & far)
             def _():
                 pass_copy(s, j).start()
 
+    def project(j):
         normed = rms_norm(embedded(j), gain1[...]).astype(BF)
         keys = jnp.dot(normed, wk[...], preferred_element_type=F32).astype(BF)
         row = lax.broadcasted_iota(jnp.int32, (quarter, LANES), 0)
@@ -185,13 +211,13 @@
         dead = (lane == 0) & (row >= length - j * quarter)
         bias = jnp.where(dead, NEG, 0.0).astype(BF)
         for p in range(HEADS // 2):
-            k_s[:, 2 * p * LANES : (2 * p + 1) * LANES] = keys[:, p * LANES : (p + 1) * LANES]
-            k_s[:, (2 * p + 1) * LANES : (2 * p + 2) * LANES] = bias
-        v_s[...] = lax.dot_general(wv[...], normed, dims_nt, preferred_element_type=F32).astype(BF)
-
-        @pl.when((j == hi) | (j == lo))
+            k_s[j, :, 2 * p * LANES : (2 * p + 1) * LANES] = keys[:, p * LANES : (p + 1) * LANES]
+            k_s[j, :, (2 * p + 1) * LANES : (2 * p + 2) * LANES] = bias
+        v_s[j] = lax.dot_general(wv[...], normed, dims_nt, preferred_element_type=F32).astype(BF)
+
+        @pl.when((j == q_sent) | (j == q_kept))
         def _():
-            slot = jnp.where(j == hi, 0, 1)
+            slot = jnp.where(j == q_sent, 0, 1)
             q_t = lax.dot_general(wq[...], normed, dims_nt, preferred_element_type=F32)
             q_t = (q_t * SCORE_SCALE).astype(BF)
             zero = jnp.zeros((head_dim, quarter), BF)
@@ -205,41 +231,66 @@
             l_s[slot] = jnp.zeros(l_s.shape[1:], F32)
             acc[slot] = jnp.zeros(acc.shape[1:], F32)
 
-        def query_step(slot, carry):
-            q = jnp.where(slot == 0, hi, lo)
-
-            @pl.when(j == q)
+    def step(t, carry):
+        last = t == cols
+        j = order(hist, jnp.minimum(t, cols - 1))
+
+        @pl.when(t < cols)
+        def _():
+            arrive(j)
+
+            @pl.when(j <= hi)
             def _():
-                attend(slot, True)
-
-            @pl.when(j < q)
+                project(j)
+
+        slot = jnp.where(last, 1, 0)
+        q = jnp.where(last, q_kept, q_sent)
+        whole = last | ((hist > 0) & (j == q_sent))
+        piece = (hist == 0) & (j <= q_sent) & (t < cols)
+        count = jnp.where(whole, q + 1, jnp.where(piece, 1, 0))
+        first = jnp.where(whole, q, j)
+
+        def unit(i, carry):
+            key = first - i
+
+            @pl.when(key == q)
             def _():
-                attend(slot, False)
-
-            @pl.when(j == 0)
+                attend(slot, key, True)
+
+            @pl.when(key < q)
             def _():
-                finish(slot, q)
+                attend(slot, key, False)
+
+            @pl.when(key == 0)
+            def _():
+                att_t = (acc[slot] / l_s[slot]).reshape(HEADS * head_dim, quarter)
+                attended = att_t.T.astype(BF)
+                hidden = embedded(q) + jnp.dot(attended, wo[...], preferred_element_type=F32)
+                hidden = hidden.astype(BF)
+
+                @pl.when(last)
+                def _():
+                    hbuf[hist] = hidden
+
+                @pl.when(t < cols)
+                def _():
+                    hstage[...] = hidden
+                    hidden_copy().start()
 
             return carry
 
-        lax.fori_loop(0, 2, query_step, 0)
+        lax.fori_loop(0, count, unit, 0)
         return carry
 
-    loads[3].wait()
-    lax.fori_loop(0, hi + 1, key_step, 0)
-    loads[4].wait()
-    loads[5].wait()
+    lax.fori_loop(0, cols + 1, step, 0)
 
     def mlp(i, carry):
         h = jnp.where(i == 0, hist, other)
-        pltpu.make_async_remote_copy(
-            src_ref=hbuf.at[h],
-            dst_ref=hbuf.at[h],
-            send_sem=hsend_sem.at[0],
-            recv_sem=hrecv_sem.at[h],
-            device_id={"cols": mate},
-            device_id_type=MESH,
-        ).wait_recv()
+
+        @pl.when(i > 0)
+        def _():
+            hidden_copy().wait_recv()
+
         hidden = hbuf[h].astype(F32)
         normed_two = rms_norm(hidden, gain2[...]).astype(BF)
         ff = wd.shape[0]
@@ -254,7 +305,7 @@
         return carry
 
     lax.fori_loop(0, batch, mlp, 0)
-    for j in reversed(range(cols)):
+    for j in range(cols):
         far_copy(j).wait_send()
 
         @pl.when(j <= mate_hi)
@@ -263,18 +314,17 @@
 
         for s in range(cols):
 
-            @pl.when(is_inner & (s // group == other) & (j <= cols - 2))
+            @pl.when(is_inner & (s // group == other))
             def _():
                 pass_copy(s, j).wait_send()
 
-    hidden_copy(0, hi).wait_send()
-    hidden_copy(1, lo).wait_send()
-
-
-def layer_call(cols, lengths, emb, gain1, gain2, w_qkv, w_out, w_in, w_down):
-    batch, full, width = emb.shape
+    hidden_copy().wait_send()
+
+
+def layer_call(cols, batch, lengths, slots, returned, gain1, gain2, w_qkv, w_out, w_in, w_down):
+    rows, cap, width = returned.shape
     assert batch == 2 and cols == 2 * batch
-    quarter = full // cols
+    quarter = slots.size // (batch * cols)
     d = width * cols
     wq_t = w_qkv[:, :d].T
     wk = w_qkv[:, d : 2 * d]
@@ -284,36 +334,41 @@
     smem = pl.BlockSpec(memory_space=pltpu.SMEM)
     weights = (wq_t, wk, wv_t, w_out, w_in, w_down)
     head_dim = d // HEADS
+    dma = pltpu.SemaphoreType.DMA
     return pl.pallas_call(
-        functools.partial(layer_kernel, cols),
+        functools.partial(layer_kernel, cols, batch),
         out_shape=jax.ShapeDtypeStruct((batch, quarter, d), BF),
-        in_specs=[smem, any_spec, vmem, vmem] + [any_spec] * 6,
+        in_specs=[smem, smem, any_spec, vmem, vmem] + [any_spec] * 6,
         out_specs=vmem,
         scratch_shapes=[
+            pltpu.VMEM((rows * cap, width), BF),
+            pltpu.VMEM((rows * cap, width), F32),
+            pltpu.VMEM((LANES, width), F32),
+            pltpu.VMEM((cols, quarter, width), BF),
             pltpu.VMEM((cols, cols, quarter, width), BF),
             pltpu.VMEM((batch, quarter, d), BF),
-            pltpu.VMEM((2, quarter, d), BF),
+            pltpu.VMEM((quarter, d), BF),
         ]
         + [pltpu.VMEM(w.shape, BF) for w in weights]
         + [
             pltpu.VMEM((2, HEADS, 4 * head_dim, quarter), BF),
-            pltpu.VMEM((quarter, 2 * d), BF),
-            pltpu.VMEM((d, quarter), BF),
+            pltpu.VMEM((cols, quarter, 2 * d), BF),
+            pltpu.VMEM((cols, d, quarter), BF),
             pltpu.VMEM((2, HEADS, 1, quarter), F32),
             pltpu.VMEM((2, HEADS, 1, quarter), F32),
             pltpu.VMEM((2, HEADS, head_dim, quarter), F32),
-            pltpu.SemaphoreType.DMA((2, cols)),
-            pltpu.SemaphoreType.DMA((cols, cols)),
-            pltpu.SemaphoreType.DMA((cols, cols)),
-            pltpu.SemaphoreType.DMA((2,)),
-            pltpu.SemaphoreType.DMA((batch,)),
-            pltpu.SemaphoreType.DMA((cols,)),
-            pltpu.SemaphoreType.DMA((6,)),
+            dma((rows,)),
+            dma((2, cols)),
+            dma((cols, cols)),
+            dma((cols, cols)),
+            dma,
+            dma,
+            dma((6,)),
         ],
         compiler_params=pltpu.CompilerParams(
             collective_id=0, has_side_effects=True, vmem_limit_bytes=60 * 1024 * 1024
         ),
-    )(lengths, emb, gain1.reshape(1, d), gain2.reshape(1, d), *weights)
+    )(lengths, slots, returned, gain1.reshape(1, d), gain2.reshape(1, d), *weights)
 
 
 def fetch_kernel(
@@ -488,7 +543,6 @@
     to_smem.start()
     to_smem.wait()
 
-    unroll = stage.shape[0]
     own = pltpu.make_async_copy(outbox.at[mr], ret_ref.at[mr], own_sem)
 
     def serve(i, carry):
@@ -496,17 +550,19 @@
         off = rows // 2 + dist * (1 - 2 * lax.rem(i, 2))
         r = lax.rem(mr + off, rows)
 
-        def some(k, carry):
-            base = k * unroll
-            g = base // LANES
-            first = base - g * LANES
-            for u in range(unroll):
-                at = asked_s[r, g, first + u]
-                stage[u : u + 1, :] = wide_tab[pl.ds(at, 1), :]
-            outbox[r, pl.ds(pl.multiple_of(base, unroll), unroll), :] = stage[...].astype(BF)
+        def some(g, count):
+            for u in range(count):
+                stage[u : u + 1, :] = wide_tab[pl.ds(asked_s[r, g, u], 1), :]
+            part = pl.ds(pl.multiple_of(g * LANES, LANES), count)
+            outbox[r, part, :] = stage[:count].astype(BF)
+
+        def full_line(g, carry):
+            some(g, LANES)
             return carry
 
-        lax.fori_loop(0, cap // unroll, some, 0)
+        lax.fori_loop(0, cap // LANES, full_line, 0)
+        if cap % LANES:
+            some(cap // LANES, cap % LANES)
 
         @pl.when(i < rows - 1)
         def _():
@@ -552,7 +608,7 @@
             pltpu.SMEM((rows, groups, LANES), jnp.int32),
             pltpu.VMEM((block_rows, width), BF),
             pltpu.VMEM((block_rows, width), F32),
-            pltpu.VMEM((32, width), F32),
+            pltpu.VMEM((LANES, width), F32),
             pltpu.VMEM((rows, cap, width), BF),
             dma((cols,)),
             dma((cols,)),
@@ -578,12 +634,9 @@
     token_count = batch_dev * full_len
     capacity = -(-(8 * token_count // (3 * row_count)) // 32) * 32
     returned, slots = fetch_call(row_count, col_count, capacity, token_ids, table)
-    slots = slots.reshape(col_count, batch_dev, quarter).transpose(1, 0, 2).reshape(-1)
-    flat = returned.reshape(row_count * capacity, -1)
-    emb = flat.at[slots].get(mode="promise_in_bounds")
-    emb = emb.reshape(batch_dev, full_len, -1)
     return layer_call(
-        col_count, lengths, emb, attn_gain, mlp_gain, w_qkv, w_out, w_in, w_down
+        col_count, batch_dev, lengths, slots, returned,
+        attn_gain, mlp_gain, w_qkv, w_out, w_in, w_down,
     )
 
 

time: 162 us -> 133 us (0.82)
  the two profiles are of different devices: /device:TPU:14 before, /device:TPU:26 now
where the time goes in v3:
time: 133 us; the launch traced here: 131 us
  Pallas kernels  124 us (93%)
  local copies, waits for them, and re-layouts  6.55 us (5%)
    pallas_call x1, Pallas kernels, layer_call(): pl.pallas_call(functools.partial(layer_kernel, cols, batch), out_shape=ja...  73.6 us
    pallas_call x1, Pallas kernels, fetch_call(): pl.pallas_call(functools.partial(fetch_kernel, rows, cols, cap), out_shap...  50.3 us
    unnamed x3, local copies, waits for them, and re-layouts  4.26 us

profile of v3, /device:TPU:26, one launch (start us, length us, event | category | flops | bytes accessed | tf_op | source)
XLA Modules:
  0.0 130.5 jit_solution(14638236731556953177)
XLA Ops:
  0.0 2.3 %fusion = (bf16[512,512]{1,0:T(8,128)(2,1)S(1)}, bf16[512,512]{1,0:T(8,128)(2,1)S(1)}, bf16[512,512]{1,0:T(8,128)(2,1)}) fusion(bf16[512,1536]{1,0:T(8,128)(2,1)} %param.13), kind=kLoop, calls=%fused_computation | loop fusion | bytes 3145728 | tf_op jit(solution)/shard_map/slice | solution.py:331
  2.3 1.0 copy.13
  3.3 1.0 copy.12
  4.3 50.3 %shard_map.91 = (bf16[8,1376,128]{2,1,0:T(8,128)(2,1)}, s32[32,128]{1,0:T(8,128)}) custom-call(s32[2,512]{1,0:T(2,128)} %ids_ref.1, bf16[16384,128]{1,0:T(8,128)(2,1)} %table_ref.1), custom_call_target="tpu_custom_call" | custom-call | tf_op jit(solution)/shard_map/pallas_call | solution.py:593
  54.6 73.6 %shard_map.92 = bf16[2,512,512]{2,1,0:T(8,128)(2,1)} custom-call(s32[2]{0:T(128)} %lens_ref.1, s32[32,128]{1,0:T(8,128)} %get-tuple-element.7.slots_ref, bf16[8,1376,128]{2,1,0:T(8,128)(2,1)} %get-tuple-element.8.raw_ref, f32[1,512]{1,0:T(1,128)} %bitcast.6, f32[1,512]{1,0:T(1,128)} %bitcast.7, bf16[512,512]{1,0:T(8,128)(2,1)} %bitcast.5, ...), custom_call_target="tpu_custom_call" | custom-call | tf_op jit(solution)/shard_map/pallas_call | solution.py:338
  128.3 2.3 %copy.15 = bf16[2,512,512]{2,1,0:T(8,128)(2,1)} copy(bf16[2,512,512]{2,1,0:T(8,128)(2,1)} %shard_map.92) | data formatting | bytes 2097152

commit v4 on v1

v4 whole, which is shorter than its diff:
```python
import functools

import jax
import jax.numpy as jnp
from jax import lax
from jax.experimental import pallas as pl
from jax.experimental.pallas import tpu as pltpu
from jax.sharding import PartitionSpec as P

HEADS = 8
LANES = 128
NEG = -1e30
SCORE_SCALE = 0.125 * 1.4426950408889634
MESH = pl.DeviceIdType.MESH
BF = jnp.bfloat16
F32 = jnp.float32


def rms_norm(values_f32, gain):
    mean_sq = jnp.mean(values_f32 * values_f32, axis=-1, keepdims=True)
    return values_f32 * lax.rsqrt(mean_sq + 1e-06) * gain


def whole_kernel(
    rows, cols, cap, ids_ref, lens_ref, table_ref, gain1, gain2, wqkv_h, wo_h, wi_h, wd_h, out_ref,
    ids_all, ids_s, slots_v, slots_s, left, right, req, asked, asked_s, tab, wide_tab, outbox, raw,
    stage, ebox, ebuf, hbuf, hstage, wqkv, wo, wi, wd, wq, wv, qm, k_s, v_s, m_s, l_s, acc,
    ids_send, ids_recv, req_send, req_recv, row_send, row_recv, tab_sem, smem_sem,
    send_sem, pass_sem, recv_sem, hsend_sem, hrecv_sem, w_sem,
):
    me = lax.axis_index("cols")
    mr = lax.axis_index("rows")
    batch, quarter = ids_ref.shape
    block_rows, width = table_ref.shape
    d = width * cols
    tiles = quarter // LANES
    lines = ids_s.shape[0]
    groups = req.shape[1]
    pieces = tab_sem.shape[0]
    piece = block_rows // pieces
    shift = block_rows.bit_length() - 1
    half = quarter // 2
    head_dim = LANES // 2
    group = cols // batch
    hist = me // group
    other = batch - 1 - hist
    inner = group - 1 + hist
    far_inner = group - 1 + other
    mate = hist * group + (group - 1 - lax.rem(me, group))
    is_inner = me == inner
    falling = hist == 0
    hi = jnp.where(is_inner, cols - 2, cols - 1)
    mate_hi = jnp.where(is_inner, cols - 1, cols - 2)
    q_sent = jnp.where(falling, hi, cols - 1 - hi)
    q_kept = cols - 1 - q_sent

    def tab_copy(i):
        part = pl.ds(i * piece, piece)
        return pltpu.make_async_copy(table_ref.at[part], tab.at[part], tab_sem.at[i])

    for i in range(pieces):
        tab_copy(i).start()
    loads = [
        pltpu.make_async_copy(src, dst, w_sem.at[i])
        for i, (src, dst) in enumerate(((wqkv_h, wqkv), (wo_h, wo), (wi_h, wi), (wd_h, wd)))
    ]

    def order(h, t):
        return jnp.where(h == 0, cols - 1 - t, t)

    def far_copy(j):
        return pltpu.make_async_remote_copy(
            src_ref=ebox.at[j],
            dst_ref=ebuf.at[me, j],
            send_sem=send_sem.at[0, j],
            recv_sem=recv_sem.at[me, j],
            device_id={"cols": far_inner},
            device_id_type=MESH,
        )

    def mate_copy(j):
        return pltpu.make_async_remote_copy(
            src_ref=ebuf.at[me, j],
            dst_ref=ebuf.at[me, j],
            send_sem=send_sem.at[1, j],
            recv_sem=recv_sem.at[me, j],
            device_id={"cols": mate},
            device_id_type=MESH,
        )

    def pass_copy(s, j):
        return pltpu.make_async_remote_copy(
            src_ref=ebuf.at[s, j],
            dst_ref=ebuf.at[s, j],
            send_sem=pass_sem.at[s, j],
            recv_sem=recv_sem.at[s, j],
            device_id={"cols": mate},
            device_id_type=MESH,
        )

    def hidden_copy():
        return pltpu.make_async_remote_copy(
            src_ref=hstage,
            dst_ref=hbuf.at[hist],
            send_sem=hsend_sem,
            recv_sem=hrecv_sem,
            device_id={"cols": q_sent},
            device_id_type=MESH,
        )

    def ids_copy(c):
        return pltpu.make_async_remote_copy(
            src_ref=ids_ref,
            dst_ref=ids_all.at[me],
            send_sem=ids_send.at[c],
            recv_sem=ids_recv.at[me],
            device_id={"cols": c},
            device_id_type=MESH,
        )

    def ids_arrival(c):
        return pltpu.make_async_remote_copy(
            src_ref=ids_ref,
            dst_ref=ids_all.at[c],
            send_sem=ids_send.at[c],
            recv_sem=ids_recv.at[c],
            device_id={"cols": c},
            device_id_type=MESH,
        )

    def req_copy(r):
        return pltpu.make_async_remote_copy(
            src_ref=req.at[r],
            dst_ref=asked.at[mr],
            send_sem=req_send.at[r],
            recv_sem=req_recv.at[mr],
            device_id={"rows": r},
            device_id_type=MESH,
        )

    def req_arrival(r):
        return pltpu.make_async_remote_copy(
            src_ref=req.at[r],
            dst_ref=asked.at[r],
            send_sem=req_send.at[r],
            recv_sem=req_recv.at[r],
            device_id={"rows": r},
            device_id_type=MESH,
        )

    def row_copy(r):
        return pltpu.make_async_remote_copy(
            src_ref=outbox.at[r],
            dst_ref=raw.at[mr],
            send_sem=row_send.at[r],
            recv_sem=row_recv.at[mr],
            device_id={"rows": r},
            device_id_type=MESH,
        )

    def row_arrival(r):
        return pltpu.make_async_remote_copy(
            src_ref=outbox.at[r],
            dst_ref=raw.at[r],
            send_sem=row_send.at[r],
            recv_sem=row_recv.at[r],
            device_id={"rows": r},
            device_id_type=MESH,
        )

    barrier = pltpu.get_barrier_semaphore()
    for off in range(1, cols):
        pl.semaphore_signal(
            barrier, inc=1, device_id={"cols": lax.rem(me + off, cols)}, device_id_type=MESH
        )
    for off in range(1, rows):
        pl.semaphore_signal(
            barrier, inc=1, device_id={"rows": lax.rem(mr + off, rows)}, device_id_type=MESH
        )
    pl.semaphore_wait(barrier, cols - 1 + rows - 1)

    for off in range(1, cols):
        ids_copy(lax.rem(me + off, cols)).start()
    for load in loads:
        load.start()
    ids_all[me] = ids_ref[...]

    step = 512
    for i in range(pieces):
        tab_copy(i).wait()

        def widen(k, carry):
            part = pl.ds(pl.multiple_of(i * piece + k * step, step), step)
            wide_tab[part, :] = tab[part, :].astype(F32)
            return carry

        lax.fori_loop(0, piece // step, widen, 0)

    for off in range(1, cols):
        ids_arrival(lax.rem(me + off, cols)).wait_recv()
    for c in range(cols):
        for b in range(batch):
            for k in range(tiles):
                line = (c * batch + b) * tiles + k
                ids_s[line : line + 1, :] = ids_all[c, b : b + 1, k * LANES : (k + 1) * LANES]
    ids = ids_s[...]
    owner = lax.shift_right_logical(ids, shift)
    offset = ids - owner * block_rows

    src_lane = lax.broadcasted_iota(jnp.int32, (LANES, 2 * LANES), 0)
    dst_lane = lax.broadcasted_iota(jnp.int32, (LANES, 2 * LANES), 1)
    before = jnp.where(src_lane < dst_lane, 1.0, 0.0).astype(BF)
    line_a = lax.broadcasted_iota(jnp.int32, (lines, lines), 0)
    line_b = lax.broadcasted_iota(jnp.int32, (lines, lines), 1)
    above = jnp.where(line_b < line_a, 1.0, 0.0).astype(BF)
    rank = jnp.zeros((lines, LANES), F32)
    for r in range(rows):
        mine = owner == r
        counts = jnp.dot(
            jnp.where(mine, 1.0, 0.0).astype(BF), before, preferred_element_type=F32
        )
        earlier = jnp.dot(above, counts[:, LANES:].astype(BF), preferred_element_type=F32)
        rank = rank + jnp.where(mine, counts[:, :LANES] + earlier, 0.0)
    rank = rank.astype(jnp.int32)
    slots_v[...] = jnp.minimum(jnp.maximum(owner * cap + rank, 0), rows * cap - 1)
    slot_group = owner * groups + lax.shift_right_logical(rank, 7)
    lane = rank - lax.shift_right_logical(rank, 7) * LANES
    high = lax.shift_right_logical(offset, 7)
    low = (offset - high * LANES).astype(F32)
    high = high.astype(F32)
    group_iota = lax.broadcasted_iota(jnp.int32, (rows * groups, LANES), 0)
    lane_iota = lax.broadcasted_iota(jnp.int32, (LANES, LANES), 0)
    for k in range(lines):
        part = slice(k * LANES, (k + 1) * LANES)
        line = slice(k, k + 1)
        left[:, part] = jnp.where(slot_group[line] == group_iota, 1.0, 0.0).astype(BF)
        hit = lane[line] == lane_iota
        right[:LANES, part] = jnp.where(hit, high[line], 0.0).astype(BF)
        right[LANES:, part] = jnp.where(hit, low[line], 0.0).astype(BF)
    found = lax.dot_general(
        left[...], right[...], (((1,), (1,)), ((), ())), preferred_element_type=F32
    )
    found = (found[:, :LANES] * LANES + found[:, LANES:]).astype(jnp.int32)
    found = jnp.minimum(jnp.maximum(found, 0), block_rows - 1)
    req[...] = found.reshape(rows, groups, LANES)

    def offset_of(i):
        return rows // 2 + (i + 1) // 2 * (1 - 2 * lax.rem(i, 2))

    def over_rows(act):
        def body(i, carry):
            act(lax.rem(mr + i + 1, rows))
            return carry

        lax.fori_loop(0, rows - 1, body, 0)

    over_rows(lambda r: req_copy(r).start())
    asked[mr] = req[mr]
    over_rows(lambda r: req_arrival(r).wait_recv())
    to_smem = pltpu.make_async_copy(asked, asked_s, smem_sem.at[0])
    slots_copy = pltpu.make_async_copy(slots_v, slots_s, smem_sem.at[1])
    to_smem.start()
    slots_copy.start()
    to_smem.wait()
    slots_copy.wait()

    def serve(i, carry):
        r = lax.rem(mr + offset_of(i), rows)

        def some(g, count):
            for u in range(count):
                stage[u : u + 1, :] = wide_tab[pl.ds(asked_s[r, g, u], 1), :]
            part = pl.ds(pl.multiple_of(g * LANES, LANES), count)
            outbox[r, part, :] = stage[:count].astype(BF)

        def full_line(g, carry):
            some(g, LANES)
            return carry

        lax.fori_loop(0, cap // LANES, full_line, 0)
        if cap % LANES:
            some(cap // LANES, cap % LANES)

        @pl.when(i < rows - 1)
        def _():
            row_copy(r).start()

        return carry

    lax.fori_loop(0, rows, serve, 0)

    loads[0].wait()
    wq[...] = wqkv[:, :d].astype(F32).T.astype(BF)
    wv[...] = wqkv[:, 2 * d :].astype(F32).T.astype(BF)
    for load in loads[1:]:
        load.wait()

    def widen_row(i, carry):
        r = lax.rem(mr + rows - offset_of(i), rows)
        part = pl.ds(pl.multiple_of(r * cap, 16), cap)

        @pl.when(i < rows - 1)
        def _():
            row_arrival(r).wait_recv()
            wide_tab[part, :] = raw[r].astype(F32)

        @pl.when(i == rows - 1)
        def _():
            wide_tab[part, :] = outbox[r].astype(F32)

        return carry

    lax.fori_loop(0, rows, widen_row, 0)


    def pick(t, carry):
        for side in range(2):
            h = other if side == 0 else hist
            j = order(h, t)
            line = (j * batch + h) * tiles
            for k in range(tiles):
                for u in range(LANES):
                    stage[u : u + 1, :] = wide_tab[pl.ds(slots_s[line + k, u], 1), :]
                part = slice(k * LANES, (k + 1) * LANES)
                if side == 0:
                    ebox[j, part, :] = stage[...].astype(BF)
                else:
                    ebuf[me, j, part, :] = stage[...].astype(BF)
            if side == 0:
                far_copy(j).start()
            else:

                @pl.when(j <= mate_hi)
                def _():
                    mate_copy(j).start()

        return carry

    lax.fori_loop(0, cols, pick, 0)
    dims_nt = (((1,), (1,)), ((), ()))
    length = lens_ref[hist]

    def embedded(j):
        parts = [ebuf[s, j] for s in range(cols)]
        return jnp.concatenate(parts, axis=1).astype(F32)

    def flash(slot, h, k_blk, v_t, q0, qn, causal):
        s = jnp.dot(k_blk, qm[slot, h, :, q0 : q0 + qn], preferred_element_type=F32)
        kn = k_blk.shape[0]
        if causal:
            key_pos = lax.broadcasted_iota(jnp.int32, (kn, qn), 0)
            query_pos = lax.broadcasted_iota(jnp.int32, (kn, qn), 1) + q0
            s = jnp.where(key_pos <= query_pos, s, NEG)
        m_old = m_s[slot, h, :, q0 : q0 + qn]
        m_new = jnp.maximum(m_old, jnp.max(s, axis=0, keepdims=True))
        probs = jnp.exp2(s - m_new)
        alpha = jnp.exp2(m_old - m_new)
        m_s[slot, h, :, q0 : q0 + qn] = m_new
        l_s[slot, h, :, q0 : q0 + qn] = l_s[slot, h, :, q0 : q0 + qn] * alpha + jnp.sum(
            probs, axis=0, keepdims=True
        )
        acc[slot, h, :, q0 : q0 + qn] = acc[slot, h, :, q0 : q0 + qn] * alpha + jnp.dot(
            v_t, probs.astype(BF), preferred_element_type=F32
        )

    def attend(slot, j, causal):
        def pair(p, carry):
            for side in range(2):
                h = 2 * p + side
                wide_p = pl.ds(pl.multiple_of(p * 2 * LANES, 2 * LANES), 2 * LANES)
                part = pl.ds(pl.multiple_of(h * head_dim, head_dim), head_dim)
                if causal:
                    flash(slot, h, k_s[j, :half, wide_p], v_s[j, part, :half], 0, half, True)
                    flash(slot, h, k_s[j, :, wide_p], v_s[j, part, :], half, half, True)
                else:
                    flash(slot, h, k_s[j, :, wide_p], v_s[j, part, :], 0, quarter, False)
            return carry

        lax.fori_loop(0, HEADS // 2, pair, 0)

    def arrive(j):
        for s in range(cols):
            far = s // group == other

            @pl.when(far | ((s != me) & (j <= hi)))
            def _():
                pass_copy(s, j).wait_recv()

            @pl.when(is_inner & far)
            def _():
                pass_copy(s, j).start()

    def project(j):
        normed = rms_norm(embedded(j), gain1[...]).astype(BF)
        keys = jnp.dot(normed, wqkv[:, d : 2 * d], preferred_element_type=F32).astype(BF)
        row = lax.broadcasted_iota(jnp.int32, (quarter, LANES), 0)
        lane = lax.broadcasted_iota(jnp.int32, (quarter, LANES), 1)
        dead = (lane == 0) & (row >= length - j * quarter)
        bias = jnp.where(dead, NEG, 0.0).astype(BF)
        for p in range(HEADS // 2):
            k_s[j, :, 2 * p * LANES : (2 * p + 1) * LANES] = keys[:, p * LANES : (p + 1) * LANES]
            k_s[j, :, (2 * p + 1) * LANES : (2 * p + 2) * LANES] = bias
        v_s[j] = lax.dot_general(wv[...], normed, dims_nt, preferred_element_type=F32).astype(BF)

        @pl.when((j == q_sent) | (j == q_kept))
        def _():
            slot = jnp.where(j == q_sent, 0, 1)
            q_t = lax.dot_general(wq[...], normed, dims_nt, preferred_element_type=F32)
            q_t = (q_t * SCORE_SCALE).astype(BF)
            zero = jnp.zeros((head_dim, quarter), BF)
            one_row = lax.broadcasted_iota(jnp.int32, (LANES, quarter), 0) == 0
            one_row = jnp.where(one_row, 1.0, 0.0).astype(BF)
            for h in range(HEADS):
                mine = q_t[h * head_dim : (h + 1) * head_dim]
                pair = (mine, zero) if h % 2 == 0 else (zero, mine)
                qm[slot, h] = jnp.concatenate(pair + (one_row,), axis=0)
            m_s[slot] = jnp.full(m_s.shape[1:], NEG, F32)
            l_s[slot] = jnp.zeros(l_s.shape[1:], F32)
            acc[slot] = jnp.zeros(acc.shape[1:], F32)

    def step(t, carry):
        last = t == cols
        j = order(hist, jnp.minimum(t, cols - 1))

        @pl.when(t < cols)
        def _():
            arrive(j)

            @pl.when((t == cols - 1) & (hist > 0) & (me != inner))
            def _():
                hidden_copy().start()

            @pl.when(j <= hi)
            def _():
                project(j)

        slot = jnp.where(last, 1, 0)
        q = jnp.where(last, q_kept, q_sent)
        whole = last | ((hist > 0) & (j == q_sent))
        piece = (hist == 0) & (j <= q_sent) & (t < cols)
        count = jnp.where(whole, q + 1, jnp.where(piece, 1, 0))
        first = jnp.where(whole, q, j)

        def unit(i, carry):
            key = first - i

            @pl.when(key == q)
            def _():
                attend(slot, key, True)

            @pl.when(key < q)
            def _():
                attend(slot, key, False)

            @pl.when(key == 0)
            def _():
                att_t = (acc[slot] / l_s[slot]).reshape(HEADS * head_dim, quarter)
                attended = att_t.T.astype(BF)
                hidden = embedded(q) + jnp.dot(attended, wo[...], preferred_element_type=F32)
                hidden = hidden.astype(BF)

                @pl.when(last)
                def _():
                    hbuf[hist] = hidden

                @pl.when(t < cols)
                def _():
                    hstage[...] = hidden

                    @pl.when(falling | is_inner)
                    def _():
                        hidden_copy().start()

            return carry

        lax.fori_loop(0, count, unit, 0)
        return carry

    lax.fori_loop(0, cols + 1, step, 0)

    def mlp(i, carry):
        h = jnp.where(i == 0, hist, other)

        @pl.when(i > 0)
        def _():
            hidden_copy().wait_recv()

        hidden = hbuf[h].astype(F32)
        normed_two = rms_norm(hidden, gain2[...]).astype(BF)
        ff = wd.shape[0]
        tile = 512
        total = hidden
        for f in range(0, ff, tile):
            gate = jnp.dot(normed_two, wi[:, f : f + tile], preferred_element_type=F32)
            up = jnp.dot(normed_two, wi[:, ff + f : ff + f + tile], preferred_element_type=F32)
            act = (gate / (1.0 + jnp.exp(-gate)) * up).astype(BF)
            total = total + jnp.dot(act, wd[f : f + tile, :], preferred_element_type=F32)
        out_ref[h] = total.astype(BF)
        return carry

    lax.fori_loop(0, batch, mlp, 0)
    for j in range(cols):
        far_copy(j).wait_send()

        @pl.when(j <= mate_hi)
        def _():
            mate_copy(j).wait_send()

        for s in range(cols):

            @pl.when(is_inner & (s // group == other))
            def _():
                pass_copy(s, j).wait_send()

    hidden_copy().wait_send()
    for off in range(1, cols):
        ids_copy(lax.rem(me + off, cols)).wait_send()
    over_rows(lambda r: req_copy(r).wait_send())
    over_rows(lambda r: row_copy(r).wait_send())


def whole_call(rows, cols, cap, token_ids, lengths, table, gain1, gain2, w_qkv, w_out, w_in, w_down):
    batch, quarter = token_ids.shape
    tokens = batch * quarter * cols
    lines = tokens // LANES
    block_rows, width = table.shape
    d = width * cols
    head_dim = d // HEADS
    assert batch == 2 and cols == 2 * batch and rows % 2 == 0
    assert block_rows & (block_rows - 1) == 0 and rows * cap <= block_rows
    groups = -(-cap // (8 * LANES)) * 8
    any_spec = pl.BlockSpec(memory_space=pl.ANY)
    vmem = pl.BlockSpec(memory_space=pltpu.VMEM)
    smem = pl.BlockSpec(memory_space=pltpu.SMEM)
    dma = pltpu.SemaphoreType.DMA
    i32 = jnp.int32
    return pl.pallas_call(
        functools.partial(whole_kernel, rows, cols, cap),
        out_shape=jax.ShapeDtypeStruct((batch, quarter, d), BF),
        in_specs=[vmem, smem, any_spec, vmem, vmem] + [any_spec] * 4,
        out_specs=vmem,
        scratch_shapes=[
            pltpu.VMEM((cols, batch, quarter), i32),
            pltpu.VMEM((lines, LANES), i32),
            pltpu.VMEM((lines, LANES), i32),
            pltpu.SMEM((lines, LANES), i32),
            pltpu.VMEM((rows * groups, tokens), BF),
            pltpu.VMEM((2 * LANES, tokens), BF),
            pltpu.VMEM((rows, groups, LANES), i32),
            pltpu.VMEM((rows, groups, LANES), i32),
            pltpu.SMEM((rows, groups, LANES), i32),
            pltpu.VMEM((block_rows, width), BF),
            pltpu.VMEM((block_rows, width), F32),
            pltpu.VMEM((rows, cap, width), BF),
            pltpu.VMEM((rows, cap, width), BF),
            pltpu.VMEM((LANES, width), F32),
            pltpu.VMEM((cols, quarter, width), BF),
            pltpu.VMEM((cols, cols, quarter, width), BF),
            pltpu.VMEM((batch, quarter, d), BF),
            pltpu.VMEM((quarter, d), BF),
            pltpu.VMEM(w_qkv.shape, BF),
            pltpu.VMEM(w_out.shape, BF),
            pltpu.VMEM(w_in.shape, BF),
            pltpu.VMEM(w_down.shape, BF),
            pltpu.VMEM((d, d), BF),
            pltpu.VMEM((d, d), BF),
            pltpu.VMEM((2, HEADS, 4 * head_dim, quarter), BF),
            pltpu.VMEM((cols, quarter, 2 * d), BF),
            pltpu.VMEM((cols, d, quarter), BF),
            pltpu.VMEM((2, HEADS, 1, quarter), F32),
            pltpu.VMEM((2, HEADS, 1, quarter), F32),
            pltpu.VMEM((2, HEADS, head_dim, quarter), F32),
            dma((cols,)),
            dma((cols,)),
            dma((rows,)),
            dma((rows,)),
            dma((rows,)),
            dma((rows,)),
            dma((4,)),
            dma((2,)),
            dma((2, cols)),
            dma((cols, cols)),
            dma((cols, cols)),
            dma,
            dma,
            dma((4,)),
        ],
        compiler_params=pltpu.CompilerParams(
            collective_id=0, has_side_effects=True, vmem_limit_bytes=63 * 1024 * 1024
        ),
    )(token_ids, lengths, table, gain1.reshape(1, d), gain2.reshape(1, d), w_qkv, w_out, w_in, w_down)


def local(token_ids, lengths, table, attn_gain, w_qkv, w_out, mlp_gain, w_in, w_down):
    batch_dev, quarter = token_ids.shape
    col_count = lax.axis_size("cols")
    row_count = lax.axis_size("rows")
    token_count = batch_dev * quarter * col_count
    capacity = -(-(8 * token_count // (3 * row_count)) // 32) * 32
    return whole_call(
        row_count, col_count, capacity, token_ids, lengths, table,
        attn_gain, mlp_gain, w_qkv, w_out, w_in, w_down,
    )


def solution(mesh):
    in_specs = (P("rows", "cols"), P("rows"), P("rows", "cols"), P(), P(), P(), P(), P(), P())
    out_specs = P("rows", "cols", None)
    return jax.shard_map(local, mesh=mesh, in_specs=in_specs, out_specs=out_specs, check_vma=False)
```

time: 191 us -> 123 us (0.64)
  the two profiles are of different devices: /device:TPU:10 before, /device:TPU:26 now
where the time goes in v4:
time: 123 us; the launch traced here: 122 us
  Pallas kernels  119 us (97%)
  local copies, waits for them, and re-layouts  2.26 us (2%)
    pallas_call x1, Pallas kernels, whole_call(): pl.pallas_call(functools.partial(whole_kernel, rows, cols, cap), out_shap...  119 us

profile of v4, /device:TPU:26, one launch (start us, length us, event | category | flops | bytes accessed | tf_op | source)
XLA Modules:
  0.0 121.6 jit_solution(16809090793238798901)
XLA Ops:
  0.0 119.3 %shard_map.91 = bf16[2,512,512]{2,1,0:T(8,128)(2,1)} custom-call(s32[2,512]{1,0:T(2,128)} %ids_ref.1, s32[2]{0:T(128)} %lens_ref.1, bf16[16384,128]{1,0:T(8,128)(2,1)} %table_ref.1, f32[1,512]{1,0:T(1,128)} %bitcast.2, f32[1,512]{1,0:T(1,128)} %bitcast.3, bf16[512,1536]{1,0:T(8,128)(2,1)} %wqkv_h.1, bf16[512,512]{1,0:T(8,128)(2,1)} %wo_h.1, ...), custom_call_target="tpu_custom_call" | custom-call | tf_op jit(solution)/shard_map/pallas_call | solution.py:537
  119.3 2.3 %copy.11 = bf16[2,512,512]{2,1,0:T(8,128)(2,1)} copy(bf16[2,512,512]{2,1,0:T(8,128)(2,1)} %shard_map.91) | data formatting | bytes 2097152

commit v5 on v4

--- a/solution.py
+++ b/solution.py
@@ -24,7 +24,7 @@
 def whole_kernel(
     rows, cols, cap, ids_ref, lens_ref, table_ref, gain1, gain2, wqkv_h, wo_h, wi_h, wd_h, out_ref,
     ids_all, ids_s, slots_v, slots_s, left, right, req, asked, asked_s, tab, wide_tab, outbox, raw,
-    stage, ebox, ebuf, hbuf, hstage, wqkv, wo, wi, wd, wq, wv, qm, k_s, v_s, m_s, l_s, acc,
+    stage, ebox, ebuf, hbuf, hstage, wqkv, wo, wi, wd, wq, wv, qm, k_s, v_s, m_s, l_s, acc, s_buf,
     ids_send, ids_recv, req_send, req_recv, row_send, row_recv, tab_sem, smem_sem,
     send_sem, pass_sem, recv_sem, hsend_sem, hrecv_sem, w_sem,
 ):
@@ -49,10 +49,12 @@
     mate = hist * group + (group - 1 - lax.rem(me, group))
     is_inner = me == inner
     falling = hist == 0
-    hi = jnp.where(is_inner, cols - 2, cols - 1)
-    mate_hi = jnp.where(is_inner, cols - 1, cols - 2)
-    q_sent = jnp.where(falling, hi, cols - 1 - hi)
-    q_kept = cols - 1 - q_sent
+    low = cols // 2 - 1
+    hi = jnp.where(is_inner, cols - 1, low)
+    mate_hi = jnp.where(is_inner, low, cols - 1)
+
+    def query_of(slot):
+        return jnp.where(is_inner, hi - slot, jnp.where(falling, hi - slot, slot))
 
     def tab_copy(i):
         part = pl.ds(i * piece, piece)
@@ -66,7 +68,8 @@
     ]
 
     def order(h, t):
-        return jnp.where(h == 0, cols - 1 - t, t)
+        falls = jnp.where(t <= low + 1, low + 1 - t, t - 1)
+        return jnp.where(t == 0, cols - 1, jnp.where(h == 0, falls, t - 1))
 
     def far_copy(j):
         return pltpu.make_async_remote_copy(
@@ -98,13 +101,23 @@
             device_id_type=MESH,
         )
 
-    def hidden_copy():
-        return pltpu.make_async_remote_copy(
-            src_ref=hstage,
+    def hidden_copy(slot):
+        return pltpu.make_async_remote_copy(
+            src_ref=hstage.at[slot],
             dst_ref=hbuf.at[hist],
-            send_sem=hsend_sem,
-            recv_sem=hrecv_sem,
-            device_id={"cols": q_sent},
+            send_sem=hsend_sem.at[slot],
+            recv_sem=hrecv_sem.at[hist],
+            device_id={"cols": query_of(slot)},
+            device_id_type=MESH,
+        )
+
+    def hidden_arrival(h):
+        return pltpu.make_async_remote_copy(
+            src_ref=hstage.at[0],
+            dst_ref=hbuf.at[h],
+            send_sem=hsend_sem.at[0],
+            recv_sem=hrecv_sem.at[h],
+            device_id={"cols": mate},
             device_id_type=MESH,
         )
 
@@ -226,7 +239,7 @@
     slot_group = owner * groups + lax.shift_right_logical(rank, 7)
     lane = rank - lax.shift_right_logical(rank, 7) * LANES
     high = lax.shift_right_logical(offset, 7)
-    low = (offset - high * LANES).astype(F32)
+    low_part = (offset - high * LANES).astype(F32)
     high = high.astype(F32)
     group_iota = lax.broadcasted_iota(jnp.int32, (rows * groups, LANES), 0)
     lane_iota = lax.broadcasted_iota(jnp.int32, (LANES, LANES), 0)
@@ -236,7 +249,7 @@
         left[:, part] = jnp.where(slot_group[line] == group_iota, 1.0, 0.0).astype(BF)
         hit = lane[line] == lane_iota
         right[:LANES, part] = jnp.where(hit, high[line], 0.0).astype(BF)
-        right[LANES:, part] = jnp.where(hit, low[line], 0.0).astype(BF)
+        right[LANES:, part] = jnp.where(hit, low_part[line], 0.0).astype(BF)
     found = lax.dot_general(
         left[...], right[...], (((1,), (1,)), ((), ())), preferred_element_type=F32
     )
@@ -344,49 +357,50 @@
         parts = [ebuf[s, j] for s in range(cols)]
         return jnp.concatenate(parts, axis=1).astype(F32)
 
-    def flash(slot, h, k_blk, v_t, q0, qn, causal):
-        s = jnp.dot(k_blk, qm[slot, h, :, q0 : q0 + qn], preferred_element_type=F32)
-        kn = k_blk.shape[0]
+    def attend(slot, j, causal):
         if causal:
-            key_pos = lax.broadcasted_iota(jnp.int32, (kn, qn), 0)
-            query_pos = lax.broadcasted_iota(jnp.int32, (kn, qn), 1) + q0
-            s = jnp.where(key_pos <= query_pos, s, NEG)
-        m_old = m_s[slot, h, :, q0 : q0 + qn]
-        m_new = jnp.maximum(m_old, jnp.max(s, axis=0, keepdims=True))
-        probs = jnp.exp2(s - m_new)
-        alpha = jnp.exp2(m_old - m_new)
-        m_s[slot, h, :, q0 : q0 + qn] = m_new
-        l_s[slot, h, :, q0 : q0 + qn] = l_s[slot, h, :, q0 : q0 + qn] * alpha + jnp.sum(
-            probs, axis=0, keepdims=True
-        )
-        acc[slot, h, :, q0 : q0 + qn] = acc[slot, h, :, q0 : q0 + qn] * alpha + jnp.dot(
-            v_t, probs.astype(BF), preferred_element_type=F32
-        )
-
-    def attend(slot, j, causal):
-        def pair(p, carry):
-            for side in range(2):
-                h = 2 * p + side
-                wide_p = pl.ds(pl.multiple_of(p * 2 * LANES, 2 * LANES), 2 * LANES)
-                part = pl.ds(pl.multiple_of(h * head_dim, head_dim), head_dim)
-                if causal:
-                    flash(slot, h, k_s[j, :half, wide_p], v_s[j, part, :half], 0, half, True)
-                    flash(slot, h, k_s[j, :, wide_p], v_s[j, part, :], half, half, True)
-                else:
-                    flash(slot, h, k_s[j, :, wide_p], v_s[j, part, :], 0, quarter, False)
-            return carry
-
-        lax.fori_loop(0, HEADS // 2, pair, 0)
+            items = [(h, n, n - half, half) for h in range(HEADS) for n in (half, quarter)]
+        else:
+            items = [(h, quarter, 0, quarter) for h in range(HEADS)]
+
+        def scores(at):
+            h, kn, q0, qn = items[at]
+            k_blk = k_s[j, :kn, (h // 2) * 2 * LANES : (h // 2 + 1) * 2 * LANES]
+            s = jnp.dot(k_blk, qm[slot, h, :, q0 : q0 + qn], preferred_element_type=F32)
+            if causal:
+                key_pos = lax.broadcasted_iota(jnp.int32, (kn, qn), 0)
+                query_pos = lax.broadcasted_iota(jnp.int32, (kn, qn), 1) + q0
+                s = jnp.where(key_pos <= query_pos, s, NEG)
+            s_buf[at % 2, :kn, :qn] = s
+            return jnp.max(s, axis=0, keepdims=True)
+
+        top = scores(0)
+        for at, (h, kn, q0, qn) in enumerate(items):
+            next_top = scores(at + 1) if at + 1 < len(items) else None
+            cut = slice(q0, q0 + qn)
+            m_old = m_s[slot, h, :, cut]
+            m_new = jnp.maximum(m_old, top)
+            probs = jnp.exp2(s_buf[at % 2, :kn, :qn] - m_new)
+            alpha = jnp.exp2(m_old - m_new)
+            m_s[slot, h, :, cut] = m_new
+            l_s[slot, h, :, cut] = l_s[slot, h, :, cut] * alpha + jnp.sum(
+                probs, axis=0, keepdims=True
+            )
+            v_t = v_s[j, h * head_dim : (h + 1) * head_dim, :kn]
+            acc[slot, h, :, cut] = acc[slot, h, :, cut] * alpha + jnp.dot(
+                v_t, probs.astype(BF), preferred_element_type=F32
+            )
+            top = next_top
 
     def arrive(j):
         for s in range(cols):
             far = s // group == other
 
-            @pl.when(far | ((s != me) & (j <= hi)))
+            @pl.when((s != me) & (j <= hi))
             def _():
                 pass_copy(s, j).wait_recv()
 
-            @pl.when(is_inner & far)
+            @pl.when(is_inner & far & (j <= low))
             def _():
                 pass_copy(s, j).start()
 
@@ -402,9 +416,9 @@
             k_s[j, :, (2 * p + 1) * LANES : (2 * p + 2) * LANES] = bias
         v_s[j] = lax.dot_general(wv[...], normed, dims_nt, preferred_element_type=F32).astype(BF)
 
-        @pl.when((j == q_sent) | (j == q_kept))
-        def _():
-            slot = jnp.where(j == q_sent, 0, 1)
+        @pl.when((j == query_of(0)) | (j == query_of(1)))
+        def _():
+            slot = jnp.where(j == query_of(0), 0, 1)
             q_t = lax.dot_general(wq[...], normed, dims_nt, preferred_element_type=F32)
             q_t = (q_t * SCORE_SCALE).astype(BF)
             zero = jnp.zeros((head_dim, quarter), BF)
@@ -419,71 +433,69 @@
             acc[slot] = jnp.zeros(acc.shape[1:], F32)
 
     def step(t, carry):
-        last = t == cols
-        j = order(hist, jnp.minimum(t, cols - 1))
-
-        @pl.when(t < cols)
+        j = order(hist, t)
+
+        @pl.when(j <= hi)
         def _():
             arrive(j)
-
-            @pl.when((t == cols - 1) & (hist > 0) & (me != inner))
-            def _():
-                hidden_copy().start()
-
-            @pl.when(j <= hi)
-            def _():
-                project(j)
-
-        slot = jnp.where(last, 1, 0)
-        q = jnp.where(last, q_kept, q_sent)
-        whole = last | ((hist > 0) & (j == q_sent))
-        piece = (hist == 0) & (j <= q_sent) & (t < cols)
-        count = jnp.where(whole, q + 1, jnp.where(piece, 1, 0))
-        first = jnp.where(whole, q, j)
-
-        def unit(i, carry):
-            key = first - i
-
-            @pl.when(key == q)
-            def _():
-                attend(slot, key, True)
-
-            @pl.when(key < q)
-            def _():
-                attend(slot, key, False)
-
-            @pl.when(key == 0)
+            project(j)
+
+        def query_step(slot, carry):
+            q = query_of(slot)
+            known = (q == cols - 1) | (falling & (q == low))
+            fresh = jnp.where(known, 1, q + 1)
+            count = jnp.where(j == q, fresh, jnp.where(known & (j < q), 1, 0))
+            last_key = jnp.where(falling & (q == low), 0, q)
+            done = jnp.where(q == cols - 1, t == cols - 1, j == last_key)
+
+            def unit(i, carry):
+                key = j - i
+
+                @pl.when(key == q)
+                def _():
+                    attend(slot, key, True)
+
+                @pl.when(key < q)
+                def _():
+                    attend(slot, key, False)
+
+                return carry
+
+            lax.fori_loop(0, count, unit, 0)
+
+            @pl.when(done)
             def _():
                 att_t = (acc[slot] / l_s[slot]).reshape(HEADS * head_dim, quarter)
                 attended = att_t.T.astype(BF)
                 hidden = embedded(q) + jnp.dot(attended, wo[...], preferred_element_type=F32)
                 hidden = hidden.astype(BF)
 
-                @pl.when(last)
+                @pl.when(q == me)
                 def _():
                     hbuf[hist] = hidden
 
-                @pl.when(t < cols)
+                @pl.when(q != me)
                 def _():
-                    hstage[...] = hidden
-
-                    @pl.when(falling | is_inner)
-                    def _():
-                        hidden_copy().start()
+                    hstage[slot] = hidden
+                    hidden_copy(slot).start()
 
             return carry
 
-        lax.fori_loop(0, count, unit, 0)
+        @pl.when(j <= hi)
+        def _():
+            lax.fori_loop(0, 2, query_step, 0)
+
         return carry
 
-    lax.fori_loop(0, cols + 1, step, 0)
+    lax.fori_loop(0, cols, step, 0)
 
     def mlp(i, carry):
-        h = jnp.where(i == 0, hist, other)
-
-        @pl.when(i > 0)
-        def _():
-            hidden_copy().wait_recv()
+        first = jnp.where(falling | is_inner, hist, other)
+        h = jnp.where(i == 0, first, batch - 1 - first)
+
+        @pl.when((h != hist) | ((query_of(0) != me) & (query_of(1) != me)))
+        def _():
+            hidden_arrival(h).wait_recv()
 
         hidden = hbuf[h].astype(F32)
         normed_two = rms_norm(hidden, gain2[...]).astype(BF)
@@ -508,11 +520,16 @@
 
         for s in range(cols):
 
-            @pl.when(is_inner & (s // group == other))
+            @pl.when(is_inner & (s // group == other) & (j <= low))
             def _():
                 pass_copy(s, j).wait_send()
 
-    hidden_copy().wait_send()
+    for slot in range(2):
+
+        @pl.when(query_of(slot) != me)
+        def _():
+            hidden_copy(slot).wait_send()
+
     for off in range(1, cols):
         ids_copy(lax.rem(me + off, cols)).wait_send()
     over_rows(lambda r: req_copy(r).wait_send())
@@ -557,7 +574,7 @@
             pltpu.VMEM((cols, quarter, width), BF),
             pltpu.VMEM((cols, cols, quarter, width), BF),
             pltpu.VMEM((batch, quarter, d), BF),
-            pltpu.VMEM((quarter, d), BF),
+            pltpu.VMEM((2, quarter, d), BF),
             pltpu.VMEM(w_qkv.shape, BF),
             pltpu.VMEM(w_out.shape, BF),
             pltpu.VMEM(w_in.shape, BF),
@@ -570,6 +587,7 @@
             pltpu.VMEM((2, HEADS, 1, quarter), F32),
             pltpu.VMEM((2, HEADS, 1, quarter), F32),
             pltpu.VMEM((2, HEADS, head_dim, quarter), F32),
+            pltpu.VMEM((2, quarter, quarter), F32),
             dma((cols,)),
             dma((cols,)),
             dma((rows,)),
@@ -581,8 +599,8 @@
             dma((2, cols)),
             dma((cols, cols)),
             dma((cols, cols)),
-            dma,
-            dma,
+            dma((2,)),
+            dma((batch,)),
             dma((4,)),
         ],
         compiler_params=pltpu.CompilerParams(

time: 123 us -> 112 us (0.911)
  the two profiles are of different devices: /device:TPU:26 before, /device:TPU:8 now
where the time goes in v5:
time: 112 us
  Pallas kernels  109 us (97%)
  local copies, waits for them, and re-layouts  2.26 us (2%)
    pallas_call x1, Pallas kernels, whole_call(): pl.pallas_call(functools.partial(whole_kernel, rows, cols, cap), out_shap...  109 us
    unnamed x1, local copies, waits for them, and re-layouts  2.26 us

profile of v5, /device:TPU:8, one launch (start us, length us, event | category | flops | bytes accessed | tf_op | source)
XLA Modules:
  0.0 111.5 jit_solution(12240145224309164711)
XLA Ops:
  0.0 109.3 %shard_map.91 = bf16[2,512,512]{2,1,0:T(8,128)(2,1)} custom-call(s32[2,512]{1,0:T(2,128)} %ids_ref.1, s32[2]{0:T(128)} %lens_ref.1, bf16[16384,128]{1,0:T(8,128)(2,1)} %table_ref.1, f32[1,512]{1,0:T(1,128)} %bitcast.2, f32[1,512]{1,0:T(1,128)} %bitcast.3, bf16[512,1536]{1,0:T(8,128)(2,1)} %wqkv_h.1, bf16[512,512]{1,0:T(8,128)(2,1)} %wo_h.1, ...), custom_call_target="tpu_custom_call" | custom-call | tf_op jit(solution)/shard_map/pallas_call | solution.py:554
  109.3 2.3 %copy.11 = bf16[2,512,512]{2,1,0:T(8,128)(2,1)} copy(bf16[2,512,512]{2,1,0:T(8,128)(2,1)} %shard_map.91) | data formatting | bytes 2097152

commit v6 on v5

--- a/solution.py
+++ b/solution.py
@@ -24,9 +24,9 @@
 def whole_kernel(
     rows, cols, cap, ids_ref, lens_ref, table_ref, gain1, gain2, wqkv_h, wo_h, wi_h, wd_h, out_ref,
     ids_all, ids_s, slots_v, slots_s, left, right, req, asked, asked_s, tab, wide_tab, outbox, raw,
-    stage, ebox, ebuf, hbuf, hstage, wqkv, wo, wi, wd, wq, wv, qm, k_s, v_s, m_s, l_s, acc, s_buf,
+    stage, ebox, ebuf, hbuf, hstage, wqkv, wo, wi, wd, wq, wv, qm, k_s, v_s, m_s, l_s, acc, s_buf, out_v, normed_s,
     ids_send, ids_recv, req_send, req_recv, row_send, row_recv, tab_sem, smem_sem,
-    send_sem, pass_sem, recv_sem, hsend_sem, hrecv_sem, w_sem,
+    send_sem, pass_sem, recv_sem, hsend_sem, hrecv_sem, w_sem, out_sem,
 ):
     me = lax.axis_index("cols")
     mr = lax.axis_index("rows")
@@ -49,12 +49,13 @@
     mate = hist * group + (group - 1 - lax.rem(me, group))
     is_inner = me == inner
     falling = hist == 0
-    low = cols // 2 - 1
-    hi = jnp.where(is_inner, cols - 1, low)
-    mate_hi = jnp.where(is_inner, low, cols - 1)
+    hi = jnp.where(is_inner, cols - 1, 0)
+    mate_hi = cols - 1 - hi
 
     def query_of(slot):
-        return jnp.where(is_inner, hi - slot, jnp.where(falling, hi - slot, slot))
+        rising = jnp.where(slot == 0, cols - 1, slot)
+        for_inner = jnp.where(falling, cols - 1 - slot, rising)
+        return jnp.where(is_inner, for_inner, -slot)
 
     def tab_copy(i):
         part = pl.ds(i * piece, piece)
@@ -67,9 +68,8 @@
         for i, (src, dst) in enumerate(((wqkv_h, wqkv), (wo_h, wo), (wi_h, wi), (wd_h, wd)))
     ]
 
-    def order(h, t):
-        falls = jnp.where(t <= low + 1, low + 1 - t, t - 1)
-        return jnp.where(t == 0, cols - 1, jnp.where(h == 0, falls, t - 1))
+    def order(t):
+        return jnp.where(t == 0, cols - 1, t - 1)
 
     def far_copy(j):
         return pltpu.make_async_remote_copy(
@@ -101,22 +101,24 @@
             device_id_type=MESH,
         )
 
-    def hidden_copy(slot):
-        return pltpu.make_async_remote_copy(
-            src_ref=hstage.at[slot],
-            dst_ref=hbuf.at[hist],
-            send_sem=hsend_sem.at[slot],
-            recv_sem=hrecv_sem.at[hist],
+    def hidden_copy(slot, p):
+        part = pl.ds(p * half, half)
+        return pltpu.make_async_remote_copy(
+            src_ref=hstage.at[slot, part],
+            dst_ref=hbuf.at[hist, part],
+            send_sem=hsend_sem.at[slot, p],
+            recv_sem=hrecv_sem.at[hist, p],
             device_id={"cols": query_of(slot)},
             device_id_type=MESH,
         )
 
-    def hidden_arrival(h):
-        return pltpu.make_async_remote_copy(
-            src_ref=hstage.at[0],
-            dst_ref=hbuf.at[h],
-            send_sem=hsend_sem.at[0],
-            recv_sem=hrecv_sem.at[h],
+    def hidden_arrival(h, p):
+        part = pl.ds(pl.multiple_of(p * half, half), half)
+        return pltpu.make_async_remote_copy(
+            src_ref=hstage.at[0, part],
+            dst_ref=hbuf.at[h, part],
+            send_sem=hsend_sem.at[0, p],
+            recv_sem=hrecv_sem.at[h, p],
             device_id={"cols": mate},
             device_id_type=MESH,
         )
@@ -161,22 +163,25 @@
             device_id_type=MESH,
         )
 
-    def row_copy(r):
-        return pltpu.make_async_remote_copy(
-            src_ref=outbox.at[r],
-            dst_ref=raw.at[mr],
-            send_sem=row_send.at[r],
-            recv_sem=row_recv.at[mr],
+    front = cap // LANES // 2 * LANES
+    spans = (pl.ds(0, front), pl.ds(front, cap - front))
+
+    def row_copy(r, p):
+        return pltpu.make_async_remote_copy(
+            src_ref=outbox.at[r, spans[p]],
+            dst_ref=raw.at[mr, spans[p]],
+            send_sem=row_send.at[r, p],
+            recv_sem=row_recv.at[mr, p],
             device_id={"rows": r},
             device_id_type=MESH,
         )
 
-    def row_arrival(r):
-        return pltpu.make_async_remote_copy(
-            src_ref=outbox.at[r],
-            dst_ref=raw.at[r],
-            send_sem=row_send.at[r],
-            recv_sem=row_recv.at[r],
+    def row_arrival(r, p):
+        return pltpu.make_async_remote_copy(
+            src_ref=outbox.at[r, spans[p]],
+            dst_ref=raw.at[r, spans[p]],
+            send_sem=row_send.at[r, p],
+            recv_sem=row_recv.at[r, p],
             device_id={"rows": r},
             device_id_type=MESH,
         )
@@ -269,38 +274,54 @@
 
     over_rows(lambda r: req_copy(r).start())
     asked[mr] = req[mr]
-    over_rows(lambda r: req_arrival(r).wait_recv())
-    to_smem = pltpu.make_async_copy(asked, asked_s, smem_sem.at[0])
     slots_copy = pltpu.make_async_copy(slots_v, slots_s, smem_sem.at[1])
-    to_smem.start()
     slots_copy.start()
-    to_smem.wait()
-    slots_copy.wait()
+
+    def some(r, g, count):
+        for u in range(count):
+            stage[u : u + 1, :] = wide_tab[pl.ds(asked_s[r, g, u], 1), :]
+        part = pl.ds(pl.multiple_of(g * LANES, LANES), count)
+        outbox[r, part, :] = stage[:count].astype(BF)
 
     def serve(i, carry):
+        back = i // rows
+        i = lax.rem(i, rows)
         r = lax.rem(mr + offset_of(i), rows)
 
-        def some(g, count):
-            for u in range(count):
-                stage[u : u + 1, :] = wide_tab[pl.ds(asked_s[r, g, u], 1), :]
-            part = pl.ds(pl.multiple_of(g * LANES, LANES), count)
-            outbox[r, part, :] = stage[:count].astype(BF)
+        @pl.when(back == 0)
+        def _():
+            @pl.when(i < rows - 1)
+            def _():
+                req_arrival(r).wait_recv()
+
+            to_smem = pltpu.make_async_copy(asked.at[r], asked_s.at[r], smem_sem.at[0])
+            to_smem.start()
+            to_smem.wait()
 
         def full_line(g, carry):
-            some(g, LANES)
+            some(r, g, LANES)
             return carry
 
-        lax.fori_loop(0, cap // LANES, full_line, 0)
-        if cap % LANES:
-            some(cap // LANES, cap % LANES)
-
-        @pl.when(i < rows - 1)
-        def _():
-            row_copy(r).start()
+        line_from = jnp.where(back == 0, 0, front // LANES)
+        line_to = jnp.where(back == 0, front // LANES, cap // LANES)
+        lax.fori_loop(line_from, line_to, full_line, 0)
+
+        @pl.when((back == 0) & (i < rows - 1))
+        def _():
+            row_copy(r, 0).start()
+
+        @pl.when(back == 1)
+        def _():
+            if cap % LANES:
+                some(r, cap // LANES, cap % LANES)
+
+            @pl.when(i < rows - 1)
+            def _():
+                row_copy(r, 1).start()
 
         return carry
 
-    lax.fori_loop(0, rows, serve, 0)
+    lax.fori_loop(0, 2 * rows, serve, 0)
 
     loads[0].wait()
     wq[...] = wqkv[:, :d].astype(F32).T.astype(BF)
@@ -314,7 +335,8 @@
 
         @pl.when(i < rows - 1)
         def _():
-            row_arrival(r).wait_recv()
+            for p in range(2):
+                row_arrival(r, p).wait_recv()
             wide_tab[part, :] = raw[r].astype(F32)
 
         @pl.when(i == rows - 1)
@@ -323,13 +345,14 @@
 
         return carry
 
+    slots_copy.wait()
     lax.fori_loop(0, rows, widen_row, 0)
 
 
     def pick(t, carry):
         for side in range(2):
             h = other if side == 0 else hist
-            j = order(h, t)
+            j = order(t)
             line = (j * batch + h) * tiles
             for k in range(tiles):
                 for u in range(LANES):
@@ -400,12 +423,13 @@
             def _():
                 pass_copy(s, j).wait_recv()
 
-            @pl.when(is_inner & far & (j <= low))
+            @pl.when(is_inner & far & (j == 0))
             def _():
                 pass_copy(s, j).start()
 
     def project(j):
         normed = rms_norm(embedded(j), gain1[...]).astype(BF)
+        normed_s[...] = normed
         keys = jnp.dot(normed, wqkv[:, d : 2 * d], preferred_element_type=F32).astype(BF)
         row = lax.broadcasted_iota(jnp.int32, (quarter, LANES), 0)
         lane = lax.broadcasted_iota(jnp.int32, (quarter, LANES), 1)
@@ -416,24 +440,23 @@
             k_s[j, :, (2 * p + 1) * LANES : (2 * p + 2) * LANES] = bias
         v_s[j] = lax.dot_general(wv[...], normed, dims_nt, preferred_element_type=F32).astype(BF)
 
-        @pl.when((j == query_of(0)) | (j == query_of(1)))
-        def _():
-            slot = jnp.where(j == query_of(0), 0, 1)
-            q_t = lax.dot_general(wq[...], normed, dims_nt, preferred_element_type=F32)
-            q_t = (q_t * SCORE_SCALE).astype(BF)
-            zero = jnp.zeros((head_dim, quarter), BF)
-            one_row = lax.broadcasted_iota(jnp.int32, (LANES, quarter), 0) == 0
-            one_row = jnp.where(one_row, 1.0, 0.0).astype(BF)
-            for h in range(HEADS):
-                mine = q_t[h * head_dim : (h + 1) * head_dim]
-                pair = (mine, zero) if h % 2 == 0 else (zero, mine)
-                qm[slot, h] = jnp.concatenate(pair + (one_row,), axis=0)
-            m_s[slot] = jnp.full(m_s.shape[1:], NEG, F32)
-            l_s[slot] = jnp.zeros(l_s.shape[1:], F32)
-            acc[slot] = jnp.zeros(acc.shape[1:], F32)
+
+    def queries(slot):
+        q_t = lax.dot_general(wq[...], normed_s[...], dims_nt, preferred_element_type=F32)
+        q_t = (q_t * SCORE_SCALE).astype(BF)
+        zero = jnp.zeros((head_dim, quarter), BF)
+        one_row = lax.broadcasted_iota(jnp.int32, (LANES, quarter), 0) == 0
+        one_row = jnp.where(one_row, 1.0, 0.0).astype(BF)
+        for h in range(HEADS):
+            mine = q_t[h * head_dim : (h + 1) * head_dim]
+            pair = (mine, zero) if h % 2 == 0 else (zero, mine)
+            qm[slot, h] = jnp.concatenate(pair + (one_row,), axis=0)
+        m_s[slot] = jnp.full(m_s.shape[1:], NEG, F32)
+        l_s[slot] = jnp.zeros(l_s.shape[1:], F32)
+        acc[slot] = jnp.zeros(acc.shape[1:], F32)
 
     def step(t, carry):
-        j = order(hist, t)
+        j = order(t)
 
         @pl.when(j <= hi)
         def _():
@@ -442,14 +465,20 @@
 
         def query_step(slot, carry):
             q = query_of(slot)
-            known = (q == cols - 1) | (falling & (q == low))
-            fresh = jnp.where(known, 1, q + 1)
-            count = jnp.where(j == q, fresh, jnp.where(known & (j < q), 1, 0))
-            last_key = jnp.where(falling & (q == low), 0, q)
-            done = jnp.where(q == cols - 1, t == cols - 1, j == last_key)
+            @pl.when(j == q)
+            def _():
+                queries(slot)
+
+            top_q = q == cols - 1
+            late = falling & is_inner & (slot == 2)
+            ready = jnp.where(late, t == cols - 1, j == q)
+            fresh = jnp.where(top_q, 1, q + 1)
+            count = jnp.where(ready, fresh, jnp.where(top_q & (j < q), 1, 0))
+            first = jnp.where(late, q, j)
+            done = jnp.where(top_q, t == cols - 1, ready)
 
             def unit(i, carry):
-                key = j - i
+                key = first - i
 
                 @pl.when(key == q)
                 def _():
@@ -465,25 +494,30 @@
 
             @pl.when(done)
             def _():
-                att_t = (acc[slot] / l_s[slot]).reshape(HEADS * head_dim, quarter)
-                attended = att_t.T.astype(BF)
-                hidden = embedded(q) + jnp.dot(attended, wo[...], preferred_element_type=F32)
-                hidden = hidden.astype(BF)
-
-                @pl.when(q == me)
-                def _():
-                    hbuf[hist] = hidden
-
-                @pl.when(q != me)
-                def _():
-                    hstage[slot] = hidden
-                    hidden_copy(slot).start()
+                for p in range(2):
+                    cut = slice(p * half, (p + 1) * half)
+                    att_t = acc[slot, :, :, cut] / l_s[slot, :, :, cut]
+                    attended = att_t.reshape(HEADS * head_dim, half).T.astype(BF)
+                    rows_in = [ebuf[s, q, cut] for s in range(cols)]
+                    hidden = jnp.concatenate(rows_in, axis=1).astype(F32) + jnp.dot(
+                        attended, wo[...], preferred_element_type=F32
+                    )
+                    hidden = hidden.astype(BF)
+
+                    @pl.when(q == me)
+                    def _():
+                        hbuf[hist, cut] = hidden
+
+                    @pl.when(q != me)
+                    def _():
+                        hstage[slot, cut] = hidden
+                        hidden_copy(slot, p).start()
 
             return carry
 
         @pl.when(j <= hi)
         def _():
-            lax.fori_loop(0, 2, query_step, 0)
+            lax.fori_loop(0, 3, query_step, 0)
 
         return carry
 
@@ -491,13 +525,17 @@
 
     def mlp(i, carry):
         first = jnp.where(falling | is_inner, hist, other)
-        h = jnp.where(i == 0, first, batch - 1 - first)
-
-        @pl.when((h != hist) | ((query_of(0) != me) & (query_of(1) != me)))
-        def _():
-            hidden_arrival(h).wait_recv()
-
-        hidden = hbuf[h].astype(F32)
+        h = jnp.where(i < 2, first, batch - 1 - first)
+        p = lax.rem(i, 2)
+        part = pl.ds(pl.multiple_of(p * half, half), half)
+
+        local = (query_of(0) == me) | (query_of(1) == me) | (query_of(2) == me)
+
+        @pl.when((h != hist) | ~local)
+        def _():
+            hidden_arrival(h, p).wait_recv()
+
+        hidden = hbuf[h, part, :].astype(F32)
         normed_two = rms_norm(hidden, gain2[...]).astype(BF)
         ff = wd.shape[0]
         tile = 512
@@ -507,10 +545,19 @@
             up = jnp.dot(normed_two, wi[:, ff + f : ff + f + tile], preferred_element_type=F32)
             act = (gate / (1.0 + jnp.exp(-gate)) * up).astype(BF)
             total = total + jnp.dot(act, wd[f : f + tile, :], preferred_element_type=F32)
-        out_ref[h] = total.astype(BF)
+        out_v[i] = total.astype(BF)
+        out_copy(i).start()
         return carry
 
-    lax.fori_loop(0, batch, mlp, 0)
+    def out_copy(i):
+        first = jnp.where(falling | is_inner, hist, other)
+        h = jnp.where(i < 2, first, batch - 1 - first)
+        part = pl.ds(pl.multiple_of(lax.rem(i, 2) * half, half), half)
+        return pltpu.make_async_copy(out_v.at[i], out_ref.at[h, part], out_sem.at[i])
+
+    lax.fori_loop(0, 2 * batch, mlp, 0)
+    for i in range(2 * batch):
+        out_copy(i).wait()
     for j in range(cols):
         far_copy(j).wait_send()
 
@@ -520,20 +567,22 @@
 
         for s in range(cols):
 
-            @pl.when(is_inner & (s // group == other) & (j <= low))
+            @pl.when(is_inner & (s // group == other) & (j == 0))
             def _():
                 pass_copy(s, j).wait_send()
 
-    for slot in range(2):
-
-        @pl.when(query_of(slot) != me)
-        def _():
-            hidden_copy(slot).wait_send()
+    for slot in range(3):
+
+        @pl.when((query_of(slot) != me) & (query_of(slot) >= 0))
+        def _():
+            for p in range(2):
+                hidden_copy(slot, p).wait_send()
 
     for off in range(1, cols):
         ids_copy(lax.rem(me + off, cols)).wait_send()
     over_rows(lambda r: req_copy(r).wait_send())
-    over_rows(lambda r: row_copy(r).wait_send())
+    for p in range(2):
+        over_rows(lambda r: row_copy(r, p).wait_send())
 
 
 def whole_call(rows, cols, cap, token_ids, lengths, table, gain1, gain2, w_qkv, w_out, w_in, w_down):
@@ -555,7 +604,7 @@
         functools.partial(whole_kernel, rows, cols, cap),
         out_shape=jax.ShapeDtypeStruct((batch, quarter, d), BF),
         in_specs=[vmem, smem, any_spec, vmem, vmem] + [any_spec] * 4,
-        out_specs=vmem,
+        out_specs=any_spec,
         scratch_shapes=[
             pltpu.VMEM((cols, batch, quarter), i32),
             pltpu.VMEM((lines, LANES), i32),
@@ -574,34 +623,37 @@
             pltpu.VMEM((cols, quarter, width), BF),
             pltpu.VMEM((cols, cols, quarter, width), BF),
             pltpu.VMEM((batch, quarter, d), BF),
-            pltpu.VMEM((2, quarter, d), BF),
+            pltpu.VMEM((3, quarter, d), BF),
             pltpu.VMEM(w_qkv.shape, BF),
             pltpu.VMEM(w_out.shape, BF),
             pltpu.VMEM(w_in.shape, BF),
             pltpu.VMEM(w_down.shape, BF),
             pltpu.VMEM((d, d), BF),
             pltpu.VMEM((d, d), BF),
-            pltpu.VMEM((2, HEADS, 4 * head_dim, quarter), BF),
+            pltpu.VMEM((3, HEADS, 4 * head_dim, quarter), BF),
             pltpu.VMEM((cols, quarter, 2 * d), BF),
             pltpu.VMEM((cols, d, quarter), BF),
-            pltpu.VMEM((2, HEADS, 1, quarter), F32),
-            pltpu.VMEM((2, HEADS, 1, quarter), F32),
-            pltpu.VMEM((2, HEADS, head_dim, quarter), F32),
+            pltpu.VMEM((3, HEADS, 1, quarter), F32),
+            pltpu.VMEM((3, HEADS, 1, quarter), F32),
+            pltpu.VMEM((3, HEADS, head_dim, quarter), F32),
             pltpu.VMEM((2, quarter, quarter), F32),
+            pltpu.VMEM((2 * batch, quarter // 2, d), BF),
+            pltpu.VMEM((quarter, d), BF),
             dma((cols,)),
             dma((cols,)),
             dma((rows,)),
             dma((rows,)),
-            dma((rows,)),
-            dma((rows,)),
+            dma((rows, 2)),
+            dma((rows, 2)),
             dma((4,)),
             dma((2,)),
             dma((2, cols)),
             dma((cols, cols)),
             dma((cols, cols)),
-            dma((2,)),
-            dma((batch,)),
+            dma((3, 2)),
+            dma((batch, 2)),
             dma((4,)),
+            dma((2 * batch,)),
         ],
         compiler_params=pltpu.CompilerParams(
             collective_id=0, has_side_effects=True, vmem_limit_bytes=63 * 1024 * 1024

time: 112 us -> 107 us (0.955)
  the two profiles are of different devices: /device:TPU:8 before, /device:TPU:26 now
where the time goes in v6:
time: 107 us; the launch traced here: 106 us
  Pallas kernels  104 us (97%)
  local copies, waits for them, and re-layouts  2.26 us (2%)
    pallas_call x1, Pallas kernels, whole_call(): pl.pallas_call(functools.partial(whole_kernel, rows, cols, cap), out_shap...  104 us
    unnamed x1, local copies, waits for them, and re-layouts  2.26 us

profile of v6, /device:TPU:26, one launch (start us, length us, event | category | flops | bytes accessed | tf_op | source)
XLA Modules:
  0.0 106.2 jit_solution(18309724586965981491)
XLA Ops:
  0.0 103.9 %shard_map.91 = bf16[2,512,512]{2,1,0:T(8,128)(2,1)} custom-call(s32[2,512]{1,0:T(2,128)} %ids_ref.1, s32[2]{0:T(128)} %lens_ref.1, bf16[16384,128]{1,0:T(8,128)(2,1)} %table_ref.1, f32[1,512]{1,0:T(1,128)} %bitcast.2, f32[1,512]{1,0:T(1,128)} %bitcast.3, bf16[512,1536]{1,0:T(8,128)(2,1)} %wqkv_h.1, bf16[512,512]{1,0:T(8,128)(2,1)} %wo_h.1, ...), custom_call_target="tpu_custom_call" | custom-call | tf_op jit(solution)/shard_map/pallas_call | solution.py:603
  103.9 2.3 %copy.11 = bf16[2,512,512]{2,1,0:T(8,128)(2,1)} copy(bf16[2,512,512]{2,1,0:T(8,128)(2,1)} %shard_map.91) | data formatting | bytes 2097152

commit v7 on v6

--- a/solution.py
+++ b/solution.py
@@ -470,7 +470,7 @@
                 queries(slot)
 
             top_q = q == cols - 1
-            late = falling & is_inner & (slot == 2)
+            late = is_inner & (q == cols // 2 - 1)
             ready = jnp.where(late, t == cols - 1, j == q)
             fresh = jnp.where(top_q, 1, q + 1)
             count = jnp.where(ready, fresh, jnp.where(top_q & (j < q), 1, 0))
@@ -538,7 +538,7 @@
         hidden = hbuf[h, part, :].astype(F32)
         normed_two = rms_norm(hidden, gain2[...]).astype(BF)
         ff = wd.shape[0]
-        tile = 512
+        tile = 1024
         total = hidden
         for f in range(0, ff, tile):
             gate = jnp.dot(normed_two, wi[:, f : f + tile], preferred_element_type=F32)

time: 107 us -> 106 us (level)
  no operation moved by 1% of the time
where the time goes in v7:
time: 106 us; the launch traced here: 105 us
  Pallas kernels  103 us (97%)
  local copies, waits for them, and re-layouts  2.26 us (2%)
    pallas_call x1, Pallas kernels, whole_call(): pl.pallas_call(functools.partial(whole_kernel, rows, cols, cap), out_shap...  103 us
    unnamed x1, local copies, waits for them, and re-layouts  2.26 us

profile of v7, /device:TPU:26, one launch (start us, length us, event | category | flops | bytes accessed | tf_op | source)
XLA Modules:
  0.0 105.1 jit_solution(8124778509539506688)
XLA Ops:
  0.0 102.9 %shard_map.91 = bf16[2,512,512]{2,1,0:T(8,128)(2,1)} custom-call(s32[2,512]{1,0:T(2,128)} %ids_ref.1, s32[2]{0:T(128)} %lens_ref.1, bf16[16384,128]{1,0:T(8,128)(2,1)} %table_ref.1, f32[1,512]{1,0:T(1,128)} %bitcast.2, f32[1,512]{1,0:T(1,128)} %bitcast.3, bf16[512,1536]{1,0:T(8,128)(2,1)} %wqkv_h.1, bf16[512,512]{1,0:T(8,128)(2,1)} %wo_h.1, ...), custom_call_target="tpu_custom_call" | custom-call | tf_op jit(solution)/shard_map/pallas_call | solution.py:603
  102.9 2.3 %copy.11 = bf16[2,512,512]{2,1,0:T(8,128)(2,1)} copy(bf16[2,512,512]{2,1,0:T(8,128)(2,1)} %shard_map.91) | data formatting | bytes 2097152
